TPU v7x, 8 devices: a whole 2x2x1 slice. The times are simulated.
8 devices in a mesh: dp: 1 (over z), tp: 2 (over y), ep: 4 (over x, core).
Axes of the slice: x: 2, y: 2, z: 1, core: 2. Of those that a mesh axis runs over, the one named last changes fastest.
Arguments:
- hidden: bfloat16 [512, 768], P(('dp', 'ep'))
- write_pos: int32 [512], P(('dp', 'ep'))
- enc_mask: int32 [512, 32], P(('dp', 'ep'))
- expert_idx: int32 [512], P(('dp', 'ep'))
- self_keys: bfloat16 [2, 512, 12, 32, 64], P(None, ('dp', 'ep'), 'tp')
- self_values: bfloat16 [2, 512, 12, 32, 64], P(None, ('dp', 'ep'), 'tp')
- cross_keys: bfloat16 [2, 512, 12, 32, 64], P(None, ('dp', 'ep'), 'tp')
- cross_values: bfloat16 [2, 512, 12, 32, 64], P(None, ('dp', 'ep'), 'tp')
- rel_bias: float32 [12, 32], P('tp')
- norm_scale: float32 [2, 3, 768], replicated
- w_query: bfloat16 [2, 768, 768], P(None, None, 'tp')
- w_key: bfloat16 [2, 768, 768], P(None, None, 'tp')
- w_value: bfloat16 [2, 768, 768], P(None, None, 'tp')
- w_out: bfloat16 [2, 768, 768], P(None, 'tp')
- w_cross_query: bfloat16 [2, 768, 768], P(None, None, 'tp')
- w_cross_out: bfloat16 [2, 768, 768], P(None, 'tp')
- dense_gate: bfloat16 [768, 3072], P(None, 'tp')
- dense_up: bfloat16 [768, 3072], P(None, 'tp')
- dense_down: bfloat16 [3072, 768], P('tp')
- router: float32 [768, 64], replicated
- exp_gate: bfloat16 [64, 768, 3072], P('ep', None, 'tp')
- exp_up: bfloat16 [64, 768, 3072], P('ep', None, 'tp')
- exp_down: bfloat16 [64, 3072, 768], P('ep', 'tp')
Outputs:
- output 1: bfloat16 [512, 768], P(('dp', 'ep'))
- output 2: bfloat16 [2, 512, 12, 32, 64], P(None, ('dp', 'ep'), 'tp')
- output 3: bfloat16 [2, 512, 12, 32, 64], P(None, ('dp', 'ep'), 'tp')
All inputs are finite; a program needn't handle non-finite values.
Results may differ from a plain program's by a relative error of at most 0.02.
Values are sent between devices in bfloat16 or wider.
A program may use at most 1 GiB of HBM per device.

v0:
```python
import functools

import jax
import jax.numpy as jnp
from jax import lax
from jax.experimental import pallas as pl
from jax.experimental.pallas import tpu as pltpu
from jax.sharding import PartitionSpec as P

EPS = 1e-6
NEG_BIG = -1e9
MESH = pl.DeviceIdType.MESH
BF16 = jnp.bfloat16
F32 = jnp.float32
VMEM_LIMIT = 63 * 1024 * 1024
SLOTS = 4


def rms_norm(h_float, scale):
    inv_rms = lax.rsqrt(jnp.mean(h_float * h_float, axis=-1, keepdims=True) + EPS)
    return (h_float * inv_rms * scale).astype(BF16)


def dot(a, b):
    return jnp.dot(a, b, preferred_element_type=F32)


def dot_t(a, b):
    return lax.dot_general(a, b, (((0,), (0,)), ((), ())), preferred_element_type=F32)


def dot_nt(a, b):
    return lax.dot_general(a, b, (((1,), (1,)), ((), ())), preferred_element_type=F32)


def fold_rows(prod):
    parts = [prod[i * 8:(i + 1) * 8] for i in range(prod.shape[0] // 8)]
    while len(parts) > 1:
        parts = [a + b for a, b in zip(parts[::2], parts[1::2])]
    return parts[0]


def score_head(q_head, keys, head, acc_ref, merge=None):
    for slot in range(keys.shape[1]):
        k_slot = keys[head, slot]
        if merge is not None:
            pos_b, k_new = merge
            k_slot = jnp.where(pos_b == jnp.asarray(slot, BF16), k_new, k_slot)
            keys[head, slot] = k_slot
        acc_ref[head, slot * 8:(slot + 1) * 8, :] = fold_rows(k_slot.astype(F32) * q_head)


def gather_scores(acc_ref, head, slots):
    total = acc_ref[head, pl.ds(0, slots, stride=8), :]
    for i in range(1, 8):
        total = total + acc_ref[head, pl.ds(i, slots, stride=8), :]
    return total


def softmax_rows(scores):
    top = jnp.max(scores, axis=0, keepdims=True)
    e = jnp.exp(scores - top)
    return (e / jnp.sum(e, axis=0, keepdims=True)).astype(BF16).astype(F32)


def context_head(p_ref, values, head, merge=None):
    total = None
    for slot in range(values.shape[1]):
        v_slot = values[head, slot]
        if merge is not None:
            pos_b, v_new = merge
            v_slot = jnp.where(pos_b == jnp.asarray(slot, BF16), v_new, v_slot)
            values[head, slot] = v_slot
        term = v_slot.astype(F32) * p_ref[head, slot:slot + 1, :]
        total = term if total is None else total + term
    return total


def self_kernel(layer, first, *refs):
    if first:
        (h_ref, pos_ref, scale_ref, rel_ref, wq_hbm, wk_hbm, wv_hbm, wo_hbm, k_hbm, v_hbm,
         part_ref, bias_ref, ko_hbm, vo_hbm,
         w_in, wo_ref, keys, values, q_t, k_t, v_t, acc_ref, p_ref, ctx_t,
         w_sem, k_sem, v_sem, ko_sem, vo_sem) = refs
    else:
        (h_ref, pos_ref, scale_ref, bias_ref, wq_hbm, wk_hbm, wv_hbm, wo_hbm, k_hbm, v_hbm, _, _,
         part_ref, ko_hbm, vo_hbm,
         w_in, wo_ref, keys, values, q_t, k_t, v_t, acc_ref, p_ref, ctx_t,
         w_sem, k_sem, v_sem, ko_sem, vo_sem) = refs
    heads, slots, head_dim, tokens = keys.shape

    w_copies = [pltpu.make_async_copy(w.at[layer], w_in.at[i], w_sem.at[i]) for i, w in enumerate((wq_hbm, wk_hbm, wv_hbm))]
    w_copies.append(pltpu.make_async_copy(wo_hbm.at[layer], wo_ref, w_sem.at[3]))

    def k_in(head):
        return pltpu.make_async_copy(k_hbm.at[layer, head], keys.at[head], k_sem.at[head])

    def v_in(head):
        return pltpu.make_async_copy(v_hbm.at[layer, head], values.at[head], v_sem.at[head])

    def k_out(head):
        return pltpu.make_async_copy(keys.at[head], ko_hbm.at[layer, head], ko_sem.at[head])

    def v_out(head):
        return pltpu.make_async_copy(values.at[head], vo_hbm.at[layer, head], vo_sem.at[head])

    for c in w_copies[:3]:
        c.start()
    for head in range(heads):
        k_in(head).start()
    for head in range(heads):
        v_in(head).start()
    w_copies[3].start()

    x = rms_norm(h_ref[...].astype(F32), scale_ref[0, layer:layer + 1, :])
    pos = pos_ref[...]
    dist = pos - lax.broadcasted_iota(jnp.int32, (slots, tokens), 0)
    valid = dist >= 0
    if first:
        bias = [jnp.zeros((slots, tokens), F32)] * heads
        for d in range(slots):
            hit = dist == d
            bias = [jnp.where(hit, rel_ref[head, d], b) for head, b in enumerate(bias)]
        for head in range(heads):
            bias_ref[head] = bias[head]
    pos_b = jnp.broadcast_to(pos.astype(F32), (head_dim, tokens)).astype(BF16)

    for i, target in enumerate((q_t, k_t, v_t)):
        w_copies[i].wait()
        proj = dot(x, w_in[i]).astype(BF16).astype(F32)
        target[...] = jnp.transpose(proj).reshape(target.shape).astype(target.dtype)

    def score_step(head, carry):
        k_in(head).wait()
        score_head(q_t[head], keys, head, acc_ref, (pos_b, k_t[head]))
        k_out(head).start()
        return carry

    lax.fori_loop(0, heads, score_step, 0)
    for head in range(heads):
        scores = jnp.where(valid, gather_scores(acc_ref, head, slots) + bias_ref[head], NEG_BIG)
        p_ref[head] = softmax_rows(scores)

    def context_step(head, carry):
        v_in(head).wait()
        ctx_t[head] = context_head(p_ref, values, head, (pos_b, v_t[head]))
        v_out(head).start()
        return carry

    lax.fori_loop(0, heads, context_step, 0)
    ctx = jnp.transpose(ctx_t[...].reshape(heads * head_dim, tokens)).astype(BF16)
    w_copies[3].wait()
    part_ref[...] = dot(ctx, wo_ref[...]).astype(BF16)
    for head in range(heads):
        k_out(head).wait()
        v_out(head).wait()


def self_attention(layer, h, pos, scale, bias, w_query, w_key, w_value, w_out, keys, values, prev=None):
    first = prev is None
    _, heads, slots, head_dim, tokens = keys.shape
    width, model = w_out.shape[1:]
    vmem = pl.BlockSpec(memory_space=pltpu.VMEM)
    hbm = pl.BlockSpec(memory_space=pl.ANY)
    smem = pl.BlockSpec(memory_space=pltpu.SMEM)
    ins = [h, pos, scale, bias, w_query, w_key, w_value, w_out, keys, values]
    in_specs = [vmem, vmem, vmem, smem if first else vmem] + [hbm] * 6
    cache = jax.ShapeDtypeStruct(keys.shape, keys.dtype)
    out_shape = [jax.ShapeDtypeStruct((tokens, model), BF16)]
    out_specs = [vmem]
    aliases = {}
    if first:
        out_shape.append(jax.ShapeDtypeStruct((heads, slots, tokens), F32))
        out_specs.append(vmem)
    else:
        ins += list(prev)
        in_specs += [hbm, hbm]
        aliases = {10: 1, 11: 2}
    out_shape += [cache, cache]
    out_specs += [hbm, hbm]
    dma = pltpu.SemaphoreType.DMA
    return pl.pallas_call(
        functools.partial(self_kernel, layer, first),
        out_shape=out_shape,
        in_specs=in_specs,
        out_specs=out_specs,
        input_output_aliases=aliases,
        scratch_shapes=[
            pltpu.VMEM((3, model, width), BF16),
            pltpu.VMEM((width, model), BF16),
            pltpu.VMEM((heads, slots, head_dim, tokens), BF16),
            pltpu.VMEM((heads, slots, head_dim, tokens), BF16),
            pltpu.VMEM((heads, head_dim, tokens), F32),
            pltpu.VMEM((heads, head_dim, tokens), BF16),
            pltpu.VMEM((heads, head_dim, tokens), BF16),
            pltpu.VMEM((heads, slots * 8, tokens), F32),
            pltpu.VMEM((heads, slots, tokens), F32),
            pltpu.VMEM((heads, head_dim, tokens), F32),
            dma((4,)), dma((heads,)), dma((heads,)), dma((heads,)), dma((heads,)),
        ],
        compiler_params=pltpu.CompilerParams(vmem_limit_bytes=VMEM_LIMIT),
        name=f"self_attention_{layer}",
    )(*ins)


def tp_exchange(src, dst, send_sem, recv_sem):
    return pltpu.make_async_remote_copy(
        src_ref=src, dst_ref=dst, send_sem=send_sem, recv_sem=recv_sem,
        device_id={"tp": 1 - lax.axis_index("tp")}, device_id_type=MESH)


def add_parts(h_float, mine, other):
    delta = (mine.astype(F32) + other.astype(F32)).astype(BF16)
    return (h_float + delta.astype(F32)).astype(BF16).astype(F32)


def cross_part(layer, x, mask, wq_copy, wq_ref, wo_copy, wo_ref, k_in, keys, v_in, values, q_t, acc_ref, p_ref, ctx_t):
    heads, slots, head_dim, tokens = keys.shape
    wq_copy.wait()
    proj = dot(x, wq_ref[...]).astype(BF16).astype(F32)
    q_t[...] = jnp.transpose(proj).reshape(heads, head_dim, tokens)

    def score_step(head, carry):
        k_in(head).wait()
        score_head(q_t[head], keys, head, acc_ref)
        return carry

    lax.fori_loop(0, heads, score_step, 0)
    valid = mask > 0
    for head in range(heads):
        p_ref[head] = softmax_rows(jnp.where(valid, gather_scores(acc_ref, head, slots), NEG_BIG))

    def context_step(head, carry):
        v_in(head).wait()
        ctx_t[head] = context_head(p_ref, values, head)
        return carry

    lax.fori_loop(0, heads, context_step, 0)
    ctx = jnp.transpose(ctx_t[...].reshape(heads * head_dim, tokens)).astype(BF16)
    wo_copy.wait()
    return dot(ctx, wo_ref[...]).astype(BF16)


def middle_kernel(layer, h_ref, part_ref, mask_ref, scale_ref, wq_hbm, wo_hbm, k_hbm, v_hbm, dg_hbm, du_hbm, dd_hbm,
                  out_ref,
                  wq_ref, wo_ref, keys, values, dg_ref, du_ref, dd_ref, q_t, acc_ref, p_ref, ctx_t, mine_ref, other_ref, prod_ref,
                  w_sem, k_sem, v_sem, send_sem, recv_sem):
    heads = keys.shape[0]

    def k_in(head):
        return pltpu.make_async_copy(k_hbm.at[layer, head], keys.at[head], k_sem.at[head])

    def v_in(head):
        return pltpu.make_async_copy(v_hbm.at[layer, head], values.at[head], v_sem.at[head])

    wq_copy = pltpu.make_async_copy(wq_hbm.at[layer], wq_ref, w_sem.at[0])
    wo_copy = pltpu.make_async_copy(wo_hbm.at[layer], wo_ref, w_sem.at[1])
    dense = [pltpu.make_async_copy(s, d, w_sem.at[2 + i]) for i, (s, d) in enumerate(((dg_hbm, dg_ref), (du_hbm, du_ref), (dd_hbm, dd_ref)))]

    barrier = pltpu.get_barrier_semaphore()
    pl.semaphore_signal(barrier, inc=1, device_id={"tp": 1 - lax.axis_index("tp")}, device_id_type=MESH)
    wq_copy.start()
    for head in range(heads):
        k_in(head).start()
    for head in range(heads):
        v_in(head).start()
    wo_copy.start()
    for c in dense:
        c.start()
    pl.semaphore_wait(barrier, 1)

    copies = [tp_exchange(part_ref if i == 0 else mine_ref.at[i - 1], other_ref.at[i], send_sem.at[i], recv_sem.at[i]) for i in range(3)]
    copies[0].start()
    copies[0].wait()
    h_float = add_parts(h_ref[...].astype(F32), part_ref[...], other_ref[0])

    x = rms_norm(h_float, scale_ref[1, layer:layer + 1, :])
    mine_ref[0] = cross_part(layer, x, mask_ref[...], wq_copy, wq_ref, wo_copy, wo_ref, k_in, keys, v_in, values, q_t, acc_ref, p_ref, ctx_t)
    copies[1].start()
    copies[1].wait()
    h_float = add_parts(h_float, mine_ref[0], other_ref[1])

    x = rms_norm(h_float, scale_ref[2, layer:layer + 1, :])
    dense[0].wait()
    dense[1].wait()
    width = dg_ref.shape[1]
    step = 512
    for c in range(0, width, step):
        gate_in = dot(x, dg_ref[:, c:c + step])
        lin_in = dot(x, du_ref[:, c:c + step])
        prod_ref[:, c:c + step] = (jax.nn.gelu(gate_in) * lin_in).astype(BF16)
    dense[2].wait()
    mine_ref[1] = dot(prod_ref[...], dd_ref[...]).astype(BF16)
    copies[2].start()
    copies[2].wait()
    out_ref[...] = add_parts(h_float, mine_ref[1], other_ref[2]).astype(BF16)


def middle(layer, h, part, mask, scale, w_query, w_out, keys, values, dense_gate, dense_up, dense_down):
    _, heads, slots, head_dim, tokens = keys.shape
    width, model = w_out.shape[1:]
    ff = dense_gate.shape[1]
    vmem = pl.BlockSpec(memory_space=pltpu.VMEM)
    hbm = pl.BlockSpec(memory_space=pl.ANY)
    dma = pltpu.SemaphoreType.DMA
    return pl.pallas_call(
        functools.partial(middle_kernel, layer),
        out_shape=jax.ShapeDtypeStruct((tokens, model), BF16),
        in_specs=[vmem] * 4 + [hbm] * 7,
        out_specs=vmem,
        scratch_shapes=[
            pltpu.VMEM((model, width), BF16),
            pltpu.VMEM((width, model), BF16),
            pltpu.VMEM((heads, slots, head_dim, tokens), BF16),
            pltpu.VMEM((heads, slots, head_dim, tokens), BF16),
            pltpu.VMEM((model, ff), BF16),
            pltpu.VMEM((model, ff), BF16),
            pltpu.VMEM((ff, model), BF16),
            pltpu.VMEM((heads, head_dim, tokens), F32),
            pltpu.VMEM((heads, slots * 8, tokens), F32),
            pltpu.VMEM((heads, slots, tokens), F32),
            pltpu.VMEM((heads, head_dim, tokens), F32),
            pltpu.VMEM((2, tokens, model), BF16),
            pltpu.VMEM((3, tokens, model), BF16),
            pltpu.VMEM((tokens, ff), BF16),
            dma((5,)), dma((heads,)), dma((heads,)), dma((3,)), dma((3,)),
        ],
        compiler_params=pltpu.CompilerParams(vmem_limit_bytes=VMEM_LIMIT, collective_id=0, has_side_effects=True),
        name="middle",
    )(h, part, mask, scale, w_query, w_out, keys, values, dense_gate, dense_up, dense_down)


def last_kernel(layer, h_ref, part_ref, mask_ref, idx_ref, scale_ref, router_ref, wq_hbm, wo_hbm, k_hbm, v_hbm, eg_hbm, eu_hbm, ed_hbm,
                out_ref,
                wq_ref, wo_ref, keys, values, eg_ref, eu_ref, ed_ref, q_t, acc_ref, p_ref, ctx_t, mine_ref, other_ref,
                place_ref, send_x, recv_x, rows_ref, y_ref, send_y, recv_y, gate_ref,
                w_sem, k_sem, v_sem, e_sem, tp_send, tp_recv, x_send, x_recv, y_send, y_recv):
    heads = keys.shape[0]
    tokens, model = h_ref.shape
    experts = router_ref.shape[0]
    groups, chunks, chunk_rows, _ = recv_x.shape
    local = experts // groups
    capacity = place_ref.shape[0] // experts
    per_chunk = local // chunks
    tp = lax.axis_index("tp")
    ep = lax.axis_index("ep")

    def peer_ep(offset):
        return lax.rem(ep + offset, groups)

    def peer_tp(offset):
        return lax.rem(tp + offset, 2)

    def k_in(head):
        return pltpu.make_async_copy(k_hbm.at[layer, head], keys.at[head], k_sem.at[head])

    def v_in(head):
        return pltpu.make_async_copy(v_hbm.at[layer, head], values.at[head], v_sem.at[head])

    def weights_in(expert, slot):
        return [pltpu.make_async_copy(s.at[expert], d.at[slot], e_sem.at[slot, i])
                for i, (s, d) in enumerate(((eg_hbm, eg_ref), (eu_hbm, eu_ref), (ed_hbm, ed_ref)))]

    wq_copy = pltpu.make_async_copy(wq_hbm.at[layer], wq_ref, w_sem.at[0])
    wo_copy = pltpu.make_async_copy(wo_hbm.at[layer], wo_ref, w_sem.at[1])

    others = [(dt, de) for dt in range(2) for de in range(groups) if dt or de]
    barrier = pltpu.get_barrier_semaphore()
    for dt, de in others:
        pl.semaphore_signal(barrier, inc=1, device_id={"tp": peer_tp(dt), "ep": peer_ep(de)}, device_id_type=MESH)
    wq_copy.start()
    for head in range(heads):
        k_in(head).start()
    for head in range(heads):
        v_in(head).start()
    wo_copy.start()
    for slot in range(SLOTS):
        for c in weights_in(slot, slot):
            c.start()
    pl.semaphore_wait(barrier, len(others))

    copies = [tp_exchange(part_ref if i == 0 else mine_ref, other_ref.at[i], tp_send.at[i], tp_recv.at[i]) for i in range(2)]
    copies[0].start()

    idx = idx_ref[...]
    onehot = (lax.broadcasted_iota(jnp.int32, (experts, tokens), 0) == idx).astype(F32)
    earlier = (lax.broadcasted_iota(jnp.int32, (tokens, tokens), 0) < lax.broadcasted_iota(jnp.int32, (tokens, tokens), 1)).astype(F32)
    counts = dot(onehot.astype(BF16), earlier.astype(BF16))
    slot_of = jnp.sum(counts * onehot, axis=0, keepdims=True).astype(jnp.int32)
    row_of = jnp.where(slot_of < capacity, idx * capacity + slot_of, -1)
    place_ref[...] = (lax.broadcasted_iota(jnp.int32, (experts * capacity, tokens), 0) == row_of).astype(F32).astype(BF16)

    copies[0].wait()
    h_float = add_parts(h_ref[...].astype(F32), part_ref[...], other_ref[0])
    x = rms_norm(h_float, scale_ref[1, layer:layer + 1, :])
    mine_ref[...] = cross_part(layer, x, mask_ref[...], wq_copy, wq_ref, wo_copy, wo_ref, k_in, keys, v_in, values, q_t, acc_ref, p_ref, ctx_t)
    copies[1].start()
    copies[1].wait()
    h_float = add_parts(h_float, mine_ref[...], other_ref[1])
    x = rms_norm(h_float, scale_ref[2, layer:layer + 1, :])

    send_x[...] = dot(place_ref[...], x).astype(BF16).reshape(send_x.shape)

    def x_copy(chunk, offset):
        return pltpu.make_async_remote_copy(
            src_ref=send_x.at[peer_ep(offset), chunk], dst_ref=recv_x.at[ep, chunk],
            send_sem=x_send.at[chunk, offset - 1], recv_sem=x_recv.at[chunk, ep],
            device_id={"ep": peer_ep(offset)}, device_id_type=MESH)

    def x_arrival(chunk, offset):
        return pltpu.make_async_remote_copy(
            src_ref=send_x.at[peer_ep(offset), chunk], dst_ref=recv_x.at[peer_ep(offset), chunk],
            send_sem=x_send.at[chunk, offset - 1], recv_sem=x_recv.at[chunk, peer_ep(offset)],
            device_id={"ep": peer_ep(offset)}, device_id_type=MESH)

    for chunk in range(chunks):
        for offset in range(1, groups):
            x_copy(chunk, offset).start()
    recv_x[ep] = send_x[ep]

    router = router_ref[...]
    high = router.astype(BF16)
    rest = router - high.astype(F32)
    mid = rest.astype(BF16)
    low = (rest - mid.astype(F32)).astype(BF16)
    logits = dot_nt(high, x) + (dot_nt(mid, x) + dot_nt(low, x))
    logits_exp = jnp.exp(logits - jnp.max(logits, axis=0, keepdims=True))
    gate = jnp.sum(logits_exp * onehot, axis=0, keepdims=True) / jnp.sum(logits_exp, axis=0, keepdims=True)
    gate_ref[...] = jnp.transpose(jnp.broadcast_to(gate, (tokens, tokens)))

    block = groups * chunk_rows
    r0 = lax.broadcasted_iota(jnp.int32, (block, block), 0)
    r1 = lax.broadcasted_iota(jnp.int32, (block, block), 1)
    group_rows = groups * capacity
    source = ((r0 % group_rows) // capacity) * chunk_rows + (r0 // group_rows) * capacity + r0 % capacity
    to_experts = (r1 == source).astype(F32).astype(BF16)
    back = ((r0 % chunk_rows) // capacity) * group_rows + (r0 // chunk_rows) * capacity + r0 % capacity
    to_groups = (r1 == back).astype(F32).astype(BF16)

    def y_copy(chunk, number):
        dt, de = others[number]
        return pltpu.make_async_remote_copy(
            src_ref=send_y.at[chunk, peer_ep(de)], dst_ref=recv_y.at[tp, ep, chunk],
            send_sem=y_send.at[chunk, number], recv_sem=y_recv.at[chunk, tp, ep],
            device_id={"tp": peer_tp(dt), "ep": peer_ep(de)}, device_id_type=MESH)

    def y_arrival(chunk, number):
        dt, de = others[number]
        return pltpu.make_async_remote_copy(
            src_ref=send_y.at[chunk, peer_ep(de)], dst_ref=recv_y.at[peer_tp(dt), peer_ep(de), chunk],
            send_sem=y_send.at[chunk, number], recv_sem=y_recv.at[chunk, peer_tp(dt), peer_ep(de)],
            device_id={"tp": peer_tp(dt), "ep": peer_ep(de)}, device_id_type=MESH)

    def expert_step(expert, carry):
        slot = lax.rem(expert, SLOTS)
        first_row = pl.multiple_of(lax.rem(expert, per_chunk) * group_rows, group_rows)
        rows = rows_ref[pl.ds(first_row, group_rows), :]
        w_copies = weights_in(expert, slot)
        w_copies[0].wait()
        gate_in = dot(rows, eg_ref[slot])
        w_copies[1].wait()
        lin_in = dot(rows, eu_ref[slot])
        product = (jax.nn.gelu(gate_in) * lin_in).astype(BF16)
        w_copies[2].wait()
        y_ref[pl.ds(first_row, group_rows), :] = dot(product, ed_ref[slot]).astype(BF16)

        @pl.when(expert + SLOTS < local)
        def _():
            for c in weights_in(expert + SLOTS, slot):
                c.start()
        return carry

    def chunk_step(chunk, carry):
        for offset in range(1, groups):
            x_arrival(chunk, offset).wait_recv()
        arrived = recv_x[:, chunk].reshape(block, model)
        rows_ref[...] = dot(to_experts, arrived).astype(BF16)
        lax.fori_loop(chunk * per_chunk, (chunk + 1) * per_chunk, expert_step, 0)
        send_y[chunk] = dot(to_groups, y_ref[...]).astype(BF16).reshape(groups, chunk_rows, model)
        for number in range(len(others)):
            y_copy(chunk, number).start()
        recv_y[tp, ep, chunk] = send_y[chunk, ep]
        return carry

    lax.fori_loop(0, chunks, chunk_step, 0)

    for chunk in range(chunks):
        for number in range(len(others)):
            y_arrival(chunk, number).wait_recv()
    returned = (recv_y[0].astype(F32) + recv_y[1].astype(F32)).astype(BF16).reshape(experts * capacity, model)
    combined = dot_t(place_ref[...], returned)
    gate_col = gate_ref[...]
    for c in range(0, model, tokens):
        delta = gate_col * combined[:, c:c + tokens]
        out_ref[:, c:c + tokens] = (h_float[:, c:c + tokens] + delta).astype(BF16)
    for chunk in range(chunks):
        for offset in range(1, groups):
            x_copy(chunk, offset).wait_send()
        for number in range(len(others)):
            y_copy(chunk, number).wait_send()


def last(layer, h, part, mask, idx, scale, router, w_query, w_out, keys, values, exp_gate, exp_up, exp_down, groups):
    _, heads, slots, head_dim, tokens = keys.shape
    width, model = w_out.shape[1:]
    local, _, ff = exp_gate.shape
    experts = router.shape[0]
    capacity = (2 * tokens + experts - 1) // experts
    chunk_rows = 16
    chunks = local * capacity // chunk_rows
    vmem = pl.BlockSpec(memory_space=pltpu.VMEM)
    hbm = pl.BlockSpec(memory_space=pl.ANY)
    dma = pltpu.SemaphoreType.DMA
    return pl.pallas_call(
        functools.partial(last_kernel, layer),
        out_shape=jax.ShapeDtypeStruct((tokens, model), BF16),
        in_specs=[vmem] * 6 + [hbm] * 7,
        out_specs=vmem,
        scratch_shapes=[
            pltpu.VMEM((model, width), BF16),
            pltpu.VMEM((width, model), BF16),
            pltpu.VMEM((heads, slots, head_dim, tokens), BF16),
            pltpu.VMEM((heads, slots, head_dim, tokens), BF16),
            pltpu.VMEM((SLOTS, model, ff), BF16),
            pltpu.VMEM((SLOTS, model, ff), BF16),
            pltpu.VMEM((SLOTS, ff, model), BF16),
            pltpu.VMEM((heads, head_dim, tokens), F32),
            pltpu.VMEM((heads, slots * 8, tokens), F32),
            pltpu.VMEM((heads, slots, tokens), F32),
            pltpu.VMEM((heads, head_dim, tokens), F32),
            pltpu.VMEM((tokens, model), BF16),
            pltpu.VMEM((2, tokens, model), BF16),
            pltpu.VMEM((experts * capacity, tokens), BF16),
            pltpu.VMEM((groups, chunks, chunk_rows, model), BF16),
            pltpu.VMEM((groups, chunks, chunk_rows, model), BF16),
            pltpu.VMEM((groups * chunk_rows, model), BF16),
            pltpu.VMEM((groups * chunk_rows, model), BF16),
            pltpu.VMEM((chunks, groups, chunk_rows, model), BF16),
            pltpu.VMEM((2, groups, chunks, chunk_rows, model), BF16),
            pltpu.VMEM((tokens, tokens), F32),
            dma((2,)), dma((heads,)), dma((heads,)), dma((SLOTS, 3)), dma((2,)), dma((2,)),
            dma((chunks, groups - 1)), dma((chunks, groups)), dma((chunks, 2 * groups - 1)), dma((chunks, 2, groups)),
        ],
        compiler_params=pltpu.CompilerParams(vmem_limit_bytes=VMEM_LIMIT, collective_id=1, has_side_effects=True),
        name="last",
    )(h, part, mask, idx, scale, router, w_query, w_out, keys, values, exp_gate, exp_up, exp_down)


def decode_body(groups, hidden, write_pos, enc_mask, expert_idx, self_keys, self_values, cross_keys, cross_values, rel_bias, norm_scale, w_query, w_key, w_value, w_out, w_cross_query, w_cross_out, dense_gate, dense_up, dense_down, router, exp_gate, exp_up, exp_down):
    def lanes(cache):
        return jnp.transpose(cache, (0, 2, 3, 4, 1))

    pos = write_pos.reshape(1, -1)
    idx = expert_idx.reshape(1, -1)
    mask = jnp.transpose(enc_mask)
    scale = jnp.transpose(norm_scale, (1, 0, 2))
    keys, values, ckeys, cvalues = map(lanes, (self_keys, self_values, cross_keys, cross_values))
    part, bias, k_out, v_out = self_attention(0, hidden, pos, scale, rel_bias, w_query, w_key, w_value, w_out, keys, values)
    h = middle(0, hidden, part, mask, scale, w_cross_query, w_cross_out, ckeys, cvalues, dense_gate, dense_up, dense_down)
    part, k_out, v_out = self_attention(1, h, pos, scale, bias, w_query, w_key, w_value, w_out, keys, values, (k_out, v_out))
    h = last(1, h, part, mask, idx, scale, jnp.transpose(router), w_cross_query, w_cross_out, ckeys, cvalues, exp_gate, exp_up, exp_down, groups)
    return h, jnp.transpose(k_out, (0, 4, 1, 2, 3)), jnp.transpose(v_out, (0, 4, 1, 2, 3))


def solution(mesh):
    batch = ('dp', 'ep')
    row_spec = P(batch, None)
    vec_spec = P(batch)
    cache_spec = P(None, batch, 'tp', None, None)
    col_spec = P(None, None, 'tp')
    out_rows = P(None, 'tp', None)
    in_specs = (row_spec, vec_spec, row_spec, vec_spec, cache_spec, cache_spec, cache_spec, cache_spec, P('tp', None), P(), col_spec, col_spec, col_spec, out_rows, col_spec, out_rows, P(None, 'tp'), P(None, 'tp'), P('tp', None), P(), P('ep', None, 'tp'), P('ep', None, 'tp'), P('ep', 'tp', None))
    out_specs = (row_spec, cache_spec, cache_spec)
    body = functools.partial(decode_body, mesh.shape['ep'])
    return jax.shard_map(body, mesh=mesh, in_specs=in_specs, out_specs=out_specs, check_vma=False)
```

profile of v0, /device:TPU:0, one launch (start us, length us, event | category | flops | bytes accessed | tf_op | source)
XLA Modules:
  0.0 97.7 jit_solution(12482269417564711935)
XLA Ops:
  0.6 8.1 %self_attention_0.1 = (bf16[128,768]{1,0:T(8,128)(2,1)}, f32[6,32,128]{2,1,0:T(8,128)}, bf16[2,6,32,64,128]{4,3,2,1,0:T(8,128)(2,1)}, bf16[2,6,32,64,128]{4,3,2,1,0:T(8,128)(2,1)}) custom-call(bf16[128,768]{1,0:T(8,128)(2,1)} %h_ref.1, s32[1,128]{1,0:T(1,128)} %bitcast.28, f32[3,2,768]{2,1,0:T(2,128)} %bitcast.21, f32[6,32]{1,0:T(8,128)} %refs_3_.1, ...), custom_call_target="tpu_custom_call" | custom-call | tf_op jit(solution)/shard_map/self_attention_0/pallas_call | solution.py:182
  8.7 24.5 %middle.1.refs_0_.h_ref = bf16[128,768]{1,0:T(8,128)(2,1)} custom-call(bf16[128,768]{1,0:T(8,128)(2,1)} %h_ref.1, bf16[128,768]{1,0:T(8,128)(2,1)} %get-tuple-element.10.part_ref, s32[32,128]{1,0:T(8,128)} %bitcast.26, f32[3,2,768]{2,1,0:T(2,128)} %bitcast.22, bf16[2,768,384]{2,1,0:T(8,128)(2,1)} %wq_hbm.3, bf16[2,384,768]{2,1,0:T(8,128)(2,1)} %wo_hbm.3, ...), custom_call_target="tpu_custom_call" | custom-call | tf_op jit(solution)/shard_map/middle/pallas_call | solution.py:306
  33.2 8.1 %self_attention_1.1 = (bf16[128,768]{1,0:T(8,128)(2,1)}, bf16[2,6,32,64,128]{4,3,2,1,0:T(8,128)(2,1)}, bf16[2,6,32,64,128]{4,3,2,1,0:T(8,128)(2,1)}) custom-call(bf16[128,768]{1,0:T(8,128)(2,1)} %middle.1.refs_0_.h_ref, s32[1,128]{1,0:T(1,128)} %bitcast.29, f32[3,2,768]{2,1,0:T(2,128)} %bitcast.23, ...), custom_call_target="tpu_custom_call", output_to_operand_aliasing={{1}: (10, {}), {2}: (11, {})} | custom-call | tf_op jit(solution)/shard_map/self_attention_1/pallas_call | solution.py:182
  41.2 54.8 %last.1 = bf16[128,768]{1,0:T(8,128)(2,1)} custom-call(bf16[128,768]{1,0:T(8,128)(2,1)} %middle.1.refs_0_.h_ref, bf16[128,768]{1,0:T(8,128)(2,1)} %get-tuple-element.14.part_ref, s32[32,128]{1,0:T(8,128)} %bitcast.27, s32[1,128]{1,0:T(1,128)} %bitcast.30, f32[3,2,768]{2,1,0:T(2,128)} %bitcast.24, f32[64,768]{1,0:T(8,128)} %bitcast.25, ...), custom_call_target="tpu_custom_call" | custom-call | tf_op jit(solution)/shard_map/last/pallas_call | solution.py:514
  96.1 1.6 %copy.31 = bf16[128,768]{1,0:T(8,128)(2,1)} copy(bf16[128,768]{1,0:T(8,128)(2,1)} %last.1) | data formatting | bytes 393216
where the time goes:
time: 97.9 us; the launch traced here: 97.7 us
  Pallas kernels  95.4 us (97%)
  local copies, waits for them, and re-layouts  1.62 us (2%)
    pallas_call x1, Pallas kernels, last(): pl.pallas_call(functools.partial(last_kernel, layer), out_shape=jax.Shape...  54.8 us
    pallas_call x1, Pallas kernels, middle(): pl.pallas_call(functools.partial(middle_kernel, layer), out_shape=jax.Sha...  24.5 us
    pallas_call x2, Pallas kernels, self_attention(): pl.pallas_call(functools.partial(self_kernel, layer, first), out_shape=ou...  16.1 us

commit v1 on v0

--- a/solution.py
+++ b/solution.py
@@ -13,7 +13,7 @@
 BF16 = jnp.bfloat16
 F32 = jnp.float32
 VMEM_LIMIT = 63 * 1024 * 1024
-SLOTS = 4
+SLOTS = 7
 
 
 def rms_norm(h_float, scale):

time: 97.9 us -> 101 us (1.032)
  Pallas kernels: 95.4 us -> 98.8 us
    pallas_call x1, Pallas kernels: 54.8 us -> 58.2 us  [last(): pl.pallas_call(functools.partial(last_kernel, layer), out_shape=jax.Shape...]
where the time goes in v1:
time: 101 us
  Pallas kernels  98.8 us (98%)
  local copies, waits for them, and re-layouts  1.62 us (2%)
    pallas_call x1, Pallas kernels, last(): pl.pallas_call(functools.partial(last_kernel, layer), out_shape=jax.Shape...  58.2 us
    pallas_call x1, Pallas kernels, middle(): pl.pallas_call(functools.partial(middle_kernel, layer), out_shape=jax.Sha...  24.5 us
    pallas_call x2, Pallas kernels, self_attention(): pl.pallas_call(functools.partial(self_kernel, layer, first), out_shape=ou...  16.1 us

profile of v1, /device:TPU:0, one launch (start us, length us, event | category | flops | bytes accessed | tf_op | source)
XLA Modules:
  0.0 101.1 jit_solution(12888612121309991433)
XLA Ops:
  0.6 8.1 %self_attention_0.1 = (bf16[128,768]{1,0:T(8,128)(2,1)}, f32[6,32,128]{2,1,0:T(8,128)}, bf16[2,6,32,64,128]{4,3,2,1,0:T(8,128)(2,1)}, bf16[2,6,32,64,128]{4,3,2,1,0:T(8,128)(2,1)}) custom-call(bf16[128,768]{1,0:T(8,128)(2,1)} %h_ref.1, s32[1,128]{1,0:T(1,128)} %bitcast.28, f32[3,2,768]{2,1,0:T(2,128)} %bitcast.21, f32[6,32]{1,0:T(8,128)} %refs_3_.1, ...), custom_call_target="tpu_custom_call" | custom-call | tf_op jit(solution)/shard_map/self_attention_0/pallas_call | solution.py:182
  8.7 24.5 %middle.1.refs_0_.h_ref = bf16[128,768]{1,0:T(8,128)(2,1)} custom-call(bf16[128,768]{1,0:T(8,128)(2,1)} %h_ref.1, bf16[128,768]{1,0:T(8,128)(2,1)} %get-tuple-element.10.part_ref, s32[32,128]{1,0:T(8,128)} %bitcast.26, f32[3,2,768]{2,1,0:T(2,128)} %bitcast.22, bf16[2,768,384]{2,1,0:T(8,128)(2,1)} %wq_hbm.3, bf16[2,384,768]{2,1,0:T(8,128)(2,1)} %wo_hbm.3, ...), custom_call_target="tpu_custom_call" | custom-call | tf_op jit(solution)/shard_map/middle/pallas_call | solution.py:306
  33.2 8.1 %self_attention_1.1 = (bf16[128,768]{1,0:T(8,128)(2,1)}, bf16[2,6,32,64,128]{4,3,2,1,0:T(8,128)(2,1)}, bf16[2,6,32,64,128]{4,3,2,1,0:T(8,128)(2,1)}) custom-call(bf16[128,768]{1,0:T(8,128)(2,1)} %middle.1.refs_0_.h_ref, s32[1,128]{1,0:T(1,128)} %bitcast.29, f32[3,2,768]{2,1,0:T(2,128)} %bitcast.23, ...), custom_call_target="tpu_custom_call", output_to_operand_aliasing={{1}: (10, {}), {2}: (11, {})} | custom-call | tf_op jit(solution)/shard_map/self_attention_1/pallas_call | solution.py:182
  41.2 58.2 %last.1 = bf16[128,768]{1,0:T(8,128)(2,1)} custom-call(bf16[128,768]{1,0:T(8,128)(2,1)} %middle.1.refs_0_.h_ref, bf16[128,768]{1,0:T(8,128)(2,1)} %get-tuple-element.14.part_ref, s32[32,128]{1,0:T(8,128)} %bitcast.27, s32[1,128]{1,0:T(1,128)} %bitcast.30, f32[3,2,768]{2,1,0:T(2,128)} %bitcast.24, f32[64,768]{1,0:T(8,128)} %bitcast.25, ...), custom_call_target="tpu_custom_call" | custom-call | tf_op jit(solution)/shard_map/last/pallas_call | solution.py:514
  99.5 1.6 %copy.31 = bf16[128,768]{1,0:T(8,128)(2,1)} copy(bf16[128,768]{1,0:T(8,128)(2,1)} %last.1) | data formatting | bytes 393216

commit v2 on v1

--- a/solution.py
+++ b/solution.py
@@ -12,8 +12,8 @@
 MESH = pl.DeviceIdType.MESH
 BF16 = jnp.bfloat16
 F32 = jnp.float32
-VMEM_LIMIT = 63 * 1024 * 1024
-SLOTS = 7
+MIB = 1024 * 1024
+SLOTS = 6
 
 
 def rms_norm(h_float, scale):
@@ -44,9 +44,9 @@
     for slot in range(keys.shape[1]):
         k_slot = keys[head, slot]
         if merge is not None:
-            pos_b, k_new = merge
+            pos_b, k_new, merged = merge
             k_slot = jnp.where(pos_b == jnp.asarray(slot, BF16), k_new, k_slot)
-            keys[head, slot] = k_slot
+            merged[head, slot] = k_slot
         acc_ref[head, slot * 8:(slot + 1) * 8, :] = fold_rows(k_slot.astype(F32) * q_head)
 
 
@@ -68,29 +68,27 @@
     for slot in range(values.shape[1]):
         v_slot = values[head, slot]
         if merge is not None:
-            pos_b, v_new = merge
+            pos_b, v_new, merged = merge
             v_slot = jnp.where(pos_b == jnp.asarray(slot, BF16), v_new, v_slot)
-            values[head, slot] = v_slot
+            merged[head, slot] = v_slot
         term = v_slot.astype(F32) * p_ref[head, slot:slot + 1, :]
         total = term if total is None else total + term
     return total
 
 
-def self_kernel(layer, first, *refs):
-    if first:
-        (h_ref, pos_ref, scale_ref, rel_ref, wq_hbm, wk_hbm, wv_hbm, wo_hbm, k_hbm, v_hbm,
-         part_ref, bias_ref, ko_hbm, vo_hbm,
-         w_in, wo_ref, keys, values, q_t, k_t, v_t, acc_ref, p_ref, ctx_t,
-         w_sem, k_sem, v_sem, ko_sem, vo_sem) = refs
-    else:
-        (h_ref, pos_ref, scale_ref, bias_ref, wq_hbm, wk_hbm, wv_hbm, wo_hbm, k_hbm, v_hbm, _, _,
-         part_ref, ko_hbm, vo_hbm,
-         w_in, wo_ref, keys, values, q_t, k_t, v_t, acc_ref, p_ref, ctx_t,
-         w_sem, k_sem, v_sem, ko_sem, vo_sem) = refs
-    heads, slots, head_dim, tokens = keys.shape
-
+def pinned(x):
+    return pltpu.with_memory_space_constraint(x, pltpu.HBM)
+
+
+def first_kernel(layer, h_hbm, pos_hbm, scale_hbm, rel_hbm, wq_hbm, wk_hbm, wv_hbm, wo_hbm, k_hbm, v_hbm,
+                 part_ref, bias_ref, ko_hbm, vo_hbm,
+                 h_ref, pos_ref, scale_ref, rel_ref, w_in, wo_ref, keys, values, q_t, k_t, v_t, acc_ref, p_ref, ctx_t,
+                 s_sem, w_sem, k_sem, v_sem, ko_sem, vo_sem):
+    heads = keys.shape[0]
+    small = [pltpu.make_async_copy(s, d, s_sem.at[i]) for i, (s, d) in enumerate(
+        ((h_hbm, h_ref), (scale_hbm, scale_ref), (pos_hbm, pos_ref), (rel_hbm, rel_ref)))]
     w_copies = [pltpu.make_async_copy(w.at[layer], w_in.at[i], w_sem.at[i]) for i, w in enumerate((wq_hbm, wk_hbm, wv_hbm))]
-    w_copies.append(pltpu.make_async_copy(wo_hbm.at[layer], wo_ref, w_sem.at[3]))
+    wo_copy = pltpu.make_async_copy(wo_hbm.at[layer], wo_ref, w_sem.at[3])
 
     def k_in(head):
         return pltpu.make_async_copy(k_hbm.at[layer, head], keys.at[head], k_sem.at[head])
@@ -98,41 +96,66 @@
     def v_in(head):
         return pltpu.make_async_copy(v_hbm.at[layer, head], values.at[head], v_sem.at[head])
 
+    for c in small + w_copies:
+        c.start()
+    for head in range(heads):
+        k_in(head).start()
+    for head in range(heads):
+        v_in(head).start(priority=1)
+    wo_copy.start(priority=1)
+
+    slots, tokens = bias_ref.shape[1:]
+    small[2].wait()
+    small[3].wait()
+    dist = pos_ref[...] - lax.broadcasted_iota(jnp.int32, (slots, tokens), 0)
+    bias = [jnp.zeros((slots, tokens), F32)] * heads
+    for d in range(slots):
+        hit = dist == d
+        bias = [jnp.where(hit, rel_ref[head, d], b) for head, b in enumerate(bias)]
+    for head in range(heads):
+        bias_ref[head] = bias[head]
+    small[0].wait()
+    small[1].wait()
+
+    self_part(layer, h_ref, pos_ref, scale_ref, bias_ref, w_in, [c.wait for c in w_copies], wo_ref, wo_copy.wait,
+              keys, values, lambda head: k_in(head).wait(), lambda head: v_in(head).wait(), keys, values,
+              part_ref, ko_hbm, vo_hbm, q_t, k_t, v_t, acc_ref, p_ref, ctx_t, ko_sem, vo_sem)
+
+
+def second_kernel(layer, h_ref, pos_ref, scale_ref, bias_ref, w_in, wo_ref, keys_in, values_in, _, __,
+                  part_ref, ko_hbm, vo_hbm,
+                  keys, values, q_t, k_t, v_t, acc_ref, p_ref, ctx_t, ko_sem, vo_sem):
+    self_part(layer, h_ref, pos_ref, scale_ref, bias_ref, w_in, [None] * 3, wo_ref, None,
+              keys_in, values_in, None, None, keys, values,
+              part_ref, ko_hbm, vo_hbm, q_t, k_t, v_t, acc_ref, p_ref, ctx_t, ko_sem, vo_sem)
+
+
+def self_part(layer, h_ref, pos_ref, scale_ref, bias_ref, w_in, w_waits, wo_ref, wo_wait,
+              keys_in, values_in, k_wait, v_wait, keys, values,
+              part_ref, ko_hbm, vo_hbm, q_t, k_t, v_t, acc_ref, p_ref, ctx_t, ko_sem, vo_sem):
+    heads, slots, head_dim, tokens = keys.shape
+
     def k_out(head):
         return pltpu.make_async_copy(keys.at[head], ko_hbm.at[layer, head], ko_sem.at[head])
 
     def v_out(head):
         return pltpu.make_async_copy(values.at[head], vo_hbm.at[layer, head], vo_sem.at[head])
 
-    for c in w_copies[:3]:
-        c.start()
-    for head in range(heads):
-        k_in(head).start()
-    for head in range(heads):
-        v_in(head).start()
-    w_copies[3].start()
-
     x = rms_norm(h_ref[...].astype(F32), scale_ref[0, layer:layer + 1, :])
     pos = pos_ref[...]
-    dist = pos - lax.broadcasted_iota(jnp.int32, (slots, tokens), 0)
-    valid = dist >= 0
-    if first:
-        bias = [jnp.zeros((slots, tokens), F32)] * heads
-        for d in range(slots):
-            hit = dist == d
-            bias = [jnp.where(hit, rel_ref[head, d], b) for head, b in enumerate(bias)]
-        for head in range(heads):
-            bias_ref[head] = bias[head]
+    valid = pos >= lax.broadcasted_iota(jnp.int32, (slots, tokens), 0)
     pos_b = jnp.broadcast_to(pos.astype(F32), (head_dim, tokens)).astype(BF16)
 
     for i, target in enumerate((q_t, k_t, v_t)):
-        w_copies[i].wait()
+        if w_waits[i] is not None:
+            w_waits[i]()
         proj = dot(x, w_in[i]).astype(BF16).astype(F32)
         target[...] = jnp.transpose(proj).reshape(target.shape).astype(target.dtype)
 
     def score_step(head, carry):
-        k_in(head).wait()
-        score_head(q_t[head], keys, head, acc_ref, (pos_b, k_t[head]))
+        if k_wait is not None:
+            k_wait(head)
+        score_head(q_t[head], keys_in, head, acc_ref, (pos_b, k_t[head], keys))
         k_out(head).start()
         return carry
 
@@ -142,65 +165,79 @@
         p_ref[head] = softmax_rows(scores)
 
     def context_step(head, carry):
-        v_in(head).wait()
-        ctx_t[head] = context_head(p_ref, values, head, (pos_b, v_t[head]))
+        if v_wait is not None:
+            v_wait(head)
+        ctx_t[head] = context_head(p_ref, values_in, head, (pos_b, v_t[head], values))
         v_out(head).start()
         return carry
 
     lax.fori_loop(0, heads, context_step, 0)
     ctx = jnp.transpose(ctx_t[...].reshape(heads * head_dim, tokens)).astype(BF16)
-    w_copies[3].wait()
+    if wo_wait is not None:
+        wo_wait()
     part_ref[...] = dot(ctx, wo_ref[...]).astype(BF16)
     for head in range(heads):
         k_out(head).wait()
         v_out(head).wait()
 
 
-def self_attention(layer, h, pos, scale, bias, w_query, w_key, w_value, w_out, keys, values, prev=None):
-    first = prev is None
+def attention_scratch(heads, slots, head_dim, tokens):
+    return [
+        pltpu.VMEM((heads, slots, head_dim, tokens), BF16),
+        pltpu.VMEM((heads, slots, head_dim, tokens), BF16),
+        pltpu.VMEM((heads, head_dim, tokens), F32),
+        pltpu.VMEM((heads, head_dim, tokens), BF16),
+        pltpu.VMEM((heads, head_dim, tokens), BF16),
+        pltpu.VMEM((heads, slots * 8, tokens), F32),
+        pltpu.VMEM((heads, slots, tokens), F32),
+        pltpu.VMEM((heads, head_dim, tokens), F32),
+    ]
+
+
+def self_first(layer, h, pos, scale, rel, w_query, w_key, w_value, w_out, keys, values):
     _, heads, slots, head_dim, tokens = keys.shape
     width, model = w_out.shape[1:]
     vmem = pl.BlockSpec(memory_space=pltpu.VMEM)
-    hbm = pl.BlockSpec(memory_space=pl.ANY)
-    smem = pl.BlockSpec(memory_space=pltpu.SMEM)
-    ins = [h, pos, scale, bias, w_query, w_key, w_value, w_out, keys, values]
-    in_specs = [vmem, vmem, vmem, smem if first else vmem] + [hbm] * 6
-    cache = jax.ShapeDtypeStruct(keys.shape, keys.dtype)
-    out_shape = [jax.ShapeDtypeStruct((tokens, model), BF16)]
-    out_specs = [vmem]
-    aliases = {}
-    if first:
-        out_shape.append(jax.ShapeDtypeStruct((heads, slots, tokens), F32))
-        out_specs.append(vmem)
-    else:
-        ins += list(prev)
-        in_specs += [hbm, hbm]
-        aliases = {10: 1, 11: 2}
-    out_shape += [cache, cache]
-    out_specs += [hbm, hbm]
+    hbm = pl.BlockSpec(memory_space=pltpu.HBM)
     dma = pltpu.SemaphoreType.DMA
+    ins = [pinned(x) for x in (h, pos, scale, rel, w_query, w_key, w_value, w_out, keys, values)]
+    cache = pltpu.HBM(keys.shape, keys.dtype)
     return pl.pallas_call(
-        functools.partial(self_kernel, layer, first),
-        out_shape=out_shape,
-        in_specs=in_specs,
-        out_specs=out_specs,
-        input_output_aliases=aliases,
+        functools.partial(first_kernel, layer),
+        out_shape=[pltpu.VMEM((tokens, model), BF16), pltpu.VMEM((heads, slots, tokens), F32), cache, cache],
+        in_specs=[hbm] * 10,
+        out_specs=[vmem, vmem, hbm, hbm],
         scratch_shapes=[
+            pltpu.VMEM((tokens, model), BF16),
+            pltpu.VMEM(pos.shape, pos.dtype),
+            pltpu.VMEM(scale.shape, F32),
+            pltpu.SMEM(rel.shape, F32),
             pltpu.VMEM((3, model, width), BF16),
             pltpu.VMEM((width, model), BF16),
-            pltpu.VMEM((heads, slots, head_dim, tokens), BF16),
-            pltpu.VMEM((heads, slots, head_dim, tokens), BF16),
-            pltpu.VMEM((heads, head_dim, tokens), F32),
-            pltpu.VMEM((heads, head_dim, tokens), BF16),
-            pltpu.VMEM((heads, head_dim, tokens), BF16),
-            pltpu.VMEM((heads, slots * 8, tokens), F32),
-            pltpu.VMEM((heads, slots, tokens), F32),
-            pltpu.VMEM((heads, head_dim, tokens), F32),
-            dma((4,)), dma((heads,)), dma((heads,)), dma((heads,)), dma((heads,)),
+        ] + attention_scratch(heads, slots, head_dim, tokens) + [
+            dma((4,)), dma((4,)), dma((heads,)), dma((heads,)), dma((heads,)), dma((heads,)),
         ],
-        compiler_params=pltpu.CompilerParams(vmem_limit_bytes=VMEM_LIMIT),
-        name=f"self_attention_{layer}",
+        compiler_params=pltpu.CompilerParams(vmem_limit_bytes=20 * MIB),
+        name="self_first",
     )(*ins)
+
+
+def self_second(layer, h, pos, scale, bias, w_in, w_out, keys_in, values_in, k_out, v_out):
+    heads, slots, head_dim, tokens = keys_in.shape
+    vmem = pl.BlockSpec(memory_space=pltpu.VMEM)
+    hbm = pl.BlockSpec(memory_space=pltpu.HBM)
+    dma = pltpu.SemaphoreType.DMA
+    cache = pltpu.HBM(k_out.shape, k_out.dtype)
+    return pl.pallas_call(
+        functools.partial(second_kernel, layer),
+        out_shape=[pltpu.VMEM(h.shape, BF16), cache, cache],
+        in_specs=[vmem] * 8 + [hbm] * 2,
+        out_specs=[vmem, hbm, hbm],
+        input_output_aliases={8: 1, 9: 2},
+        scratch_shapes=attention_scratch(heads, slots, head_dim, tokens) + [dma((heads,)), dma((heads,))],
+        compiler_params=pltpu.CompilerParams(vmem_limit_bytes=20 * MIB),
+        name="self_second",
+    )(h, pos, scale, bias, w_in, w_out, keys_in, values_in, pinned(k_out), pinned(v_out))
 
 
 def tp_exchange(src, dst, send_sem, recv_sem):
@@ -241,11 +278,17 @@
     return dot(ctx, wo_ref[...]).astype(BF16)
 
 
-def middle_kernel(layer, h_ref, part_ref, mask_ref, scale_ref, wq_hbm, wo_hbm, k_hbm, v_hbm, dg_hbm, du_hbm, dd_hbm,
-                  out_ref,
-                  wq_ref, wo_ref, keys, values, dg_ref, du_ref, dd_ref, q_t, acc_ref, p_ref, ctx_t, mine_ref, other_ref, prod_ref,
-                  w_sem, k_sem, v_sem, send_sem, recv_sem):
+def middle_kernel(layer, part_ref, h_hbm, mask_hbm, scale_hbm, pos_hbm, wq_hbm, wo_hbm, k_hbm, v_hbm, dg_hbm, du_hbm, dd_hbm,
+                  nq_hbm, nk_hbm, nv_hbm, no_hbm, nkeys_hbm, nvalues_hbm,
+                  out_ref, pos_ref, scale_ref, nw_ref, nwo_ref, nkeys_ref, nvalues_ref,
+                  h_ref, mask_ref, wq_ref, wo_ref, keys, values, dg_ref, du_ref, dd_ref, q_t, acc_ref, p_ref, ctx_t, mine_ref, other_ref, prod_ref,
+                  w_sem, k_sem, v_sem, send_sem, recv_sem, s_sem, n_sem):
     heads = keys.shape[0]
+    small = [pltpu.make_async_copy(s, d, s_sem.at[i]) for i, (s, d) in enumerate(
+        ((h_hbm, h_ref), (mask_hbm, mask_ref), (scale_hbm, scale_ref), (pos_hbm, pos_ref)))]
+    following = [pltpu.make_async_copy(s, d, n_sem.at[i]) for i, (s, d) in enumerate(
+        ((nq_hbm.at[layer + 1], nw_ref.at[0]), (nk_hbm.at[layer + 1], nw_ref.at[1]), (nv_hbm.at[layer + 1], nw_ref.at[2]),
+         (no_hbm.at[layer + 1], nwo_ref), (nkeys_hbm.at[layer + 1], nkeys_ref), (nvalues_hbm.at[layer + 1], nvalues_ref)))]
 
     def k_in(head):
         return pltpu.make_async_copy(k_hbm.at[layer, head], keys.at[head], k_sem.at[head])
@@ -259,18 +302,22 @@
 
     barrier = pltpu.get_barrier_semaphore()
     pl.semaphore_signal(barrier, inc=1, device_id={"tp": 1 - lax.axis_index("tp")}, device_id_type=MESH)
+    for c in small:
+        c.start()
     wq_copy.start()
     for head in range(heads):
         k_in(head).start()
     for head in range(heads):
-        v_in(head).start()
-    wo_copy.start()
-    for c in dense:
-        c.start()
+        v_in(head).start(priority=1)
+    wo_copy.start(priority=1)
+    for c in dense + following:
+        c.start(priority=1)
     pl.semaphore_wait(barrier, 1)
 
     copies = [tp_exchange(part_ref if i == 0 else mine_ref.at[i - 1], other_ref.at[i], send_sem.at[i], recv_sem.at[i]) for i in range(3)]
     copies[0].start()
+    for c in small:
+        c.wait()
     copies[0].wait()
     h_float = add_parts(h_ref[...].astype(F32), part_ref[...], other_ref[0])
 
@@ -294,21 +341,29 @@
     copies[2].start()
     copies[2].wait()
     out_ref[...] = add_parts(h_float, mine_ref[1], other_ref[2]).astype(BF16)
-
-
-def middle(layer, h, part, mask, scale, w_query, w_out, keys, values, dense_gate, dense_up, dense_down):
+    for c in following:
+        c.wait()
+
+
+def middle(layer, part, h, mask, scale, pos, w_query, w_out, keys, values, dense_gate, dense_up, dense_down, following):
     _, heads, slots, head_dim, tokens = keys.shape
     width, model = w_out.shape[1:]
     ff = dense_gate.shape[1]
     vmem = pl.BlockSpec(memory_space=pltpu.VMEM)
-    hbm = pl.BlockSpec(memory_space=pl.ANY)
+    hbm = pl.BlockSpec(memory_space=pltpu.HBM)
     dma = pltpu.SemaphoreType.DMA
+    cache = pltpu.VMEM((heads, slots, head_dim, tokens), BF16)
     return pl.pallas_call(
         functools.partial(middle_kernel, layer),
-        out_shape=jax.ShapeDtypeStruct((tokens, model), BF16),
-        in_specs=[vmem] * 4 + [hbm] * 7,
-        out_specs=vmem,
+        out_shape=[
+            pltpu.VMEM((tokens, model), BF16), pltpu.VMEM(pos.shape, pos.dtype), pltpu.VMEM(scale.shape, F32),
+            pltpu.VMEM((3, model, width), BF16), pltpu.VMEM((width, model), BF16), cache, cache,
+        ],
+        in_specs=[vmem] + [hbm] * 17,
+        out_specs=[vmem] * 7,
         scratch_shapes=[
+            pltpu.VMEM((tokens, model), BF16),
+            pltpu.VMEM(mask.shape, mask.dtype),
             pltpu.VMEM((model, width), BF16),
             pltpu.VMEM((width, model), BF16),
             pltpu.VMEM((heads, slots, head_dim, tokens), BF16),
@@ -323,21 +378,23 @@
             pltpu.VMEM((2, tokens, model), BF16),
             pltpu.VMEM((3, tokens, model), BF16),
             pltpu.VMEM((tokens, ff), BF16),
-            dma((5,)), dma((heads,)), dma((heads,)), dma((3,)), dma((3,)),
+            dma((5,)), dma((heads,)), dma((heads,)), dma((3,)), dma((3,)), dma((4,)), dma((6,)),
         ],
-        compiler_params=pltpu.CompilerParams(vmem_limit_bytes=VMEM_LIMIT, collective_id=0, has_side_effects=True),
+        compiler_params=pltpu.CompilerParams(vmem_limit_bytes=26 * MIB, collective_id=0, has_side_effects=True),
         name="middle",
-    )(h, part, mask, scale, w_query, w_out, keys, values, dense_gate, dense_up, dense_down)
-
-
-def last_kernel(layer, h_ref, part_ref, mask_ref, idx_ref, scale_ref, router_ref, wq_hbm, wo_hbm, k_hbm, v_hbm, eg_hbm, eu_hbm, ed_hbm,
+    )(part, *map(pinned, (h, mask, scale, pos, w_query, w_out, keys, values, dense_gate, dense_up, dense_down) + following))
+
+
+def last_kernel(layer, h_ref, part_ref, mask_hbm, idx_hbm, scale_hbm, router_hbm, wq_hbm, wo_hbm, k_hbm, v_hbm, eg_hbm, eu_hbm, ed_hbm,
                 out_ref,
-                wq_ref, wo_ref, keys, values, eg_ref, eu_ref, ed_ref, q_t, acc_ref, p_ref, ctx_t, mine_ref, other_ref,
+                mask_ref, idx_ref, scale_ref, router_ref, wq_ref, wo_ref, keys, values, eg_ref, eu_ref, ed_ref, q_t, acc_ref, p_ref, ctx_t, mine_ref, other_ref,
                 place_ref, send_x, recv_x, rows_ref, y_ref, send_y, recv_y, gate_ref,
-                w_sem, k_sem, v_sem, e_sem, tp_send, tp_recv, x_send, x_recv, y_send, y_recv):
+                w_sem, k_sem, v_sem, e_sem, tp_send, tp_recv, x_send, x_recv, y_send, y_recv, s_sem):
     heads = keys.shape[0]
     tokens, model = h_ref.shape
     experts = router_ref.shape[0]
+    small = [pltpu.make_async_copy(s, d, s_sem.at[i]) for i, (s, d) in enumerate(
+        ((mask_hbm, mask_ref), (idx_hbm, idx_ref), (scale_hbm, scale_ref), (router_hbm, router_ref)))]
     groups, chunks, chunk_rows, _ = recv_x.shape
     local = experts // groups
     capacity = place_ref.shape[0] // experts
@@ -368,6 +425,8 @@
     barrier = pltpu.get_barrier_semaphore()
     for dt, de in others:
         pl.semaphore_signal(barrier, inc=1, device_id={"tp": peer_tp(dt), "ep": peer_ep(de)}, device_id_type=MESH)
+    for c in small:
+        c.start()
     wq_copy.start()
     for head in range(heads):
         k_in(head).start()
@@ -376,12 +435,14 @@
     wo_copy.start()
     for slot in range(SLOTS):
         for c in weights_in(slot, slot):
-            c.start()
+            c.start(priority=1)
     pl.semaphore_wait(barrier, len(others))
 
     copies = [tp_exchange(part_ref if i == 0 else mine_ref, other_ref.at[i], tp_send.at[i], tp_recv.at[i]) for i in range(2)]
     copies[0].start()
 
+    for c in small:
+        c.wait()
     idx = idx_ref[...]
     onehot = (lax.broadcasted_iota(jnp.int32, (experts, tokens), 0) == idx).astype(F32)
     earlier = (lax.broadcasted_iota(jnp.int32, (tokens, tokens), 0) < lax.broadcasted_iota(jnp.int32, (tokens, tokens), 1)).astype(F32)
@@ -467,7 +528,7 @@
         @pl.when(expert + SLOTS < local)
         def _():
             for c in weights_in(expert + SLOTS, slot):
-                c.start()
+                c.start(priority=1)
         return carry
 
     def chunk_step(chunk, carry):
@@ -509,14 +570,18 @@
     chunk_rows = 16
     chunks = local * capacity // chunk_rows
     vmem = pl.BlockSpec(memory_space=pltpu.VMEM)
-    hbm = pl.BlockSpec(memory_space=pl.ANY)
+    hbm = pl.BlockSpec(memory_space=pltpu.HBM)
     dma = pltpu.SemaphoreType.DMA
     return pl.pallas_call(
         functools.partial(last_kernel, layer),
-        out_shape=jax.ShapeDtypeStruct((tokens, model), BF16),
-        in_specs=[vmem] * 6 + [hbm] * 7,
+        out_shape=pltpu.VMEM((tokens, model), BF16),
+        in_specs=[vmem] * 2 + [hbm] * 11,
         out_specs=vmem,
         scratch_shapes=[
+            pltpu.VMEM(mask.shape, mask.dtype),
+            pltpu.VMEM(idx.shape, idx.dtype),
+            pltpu.VMEM(scale.shape, F32),
+            pltpu.VMEM(router.shape, F32),
             pltpu.VMEM((model, width), BF16),
             pltpu.VMEM((width, model), BF16),
             pltpu.VMEM((heads, slots, head_dim, tokens), BF16),
@@ -539,11 +604,11 @@
             pltpu.VMEM((2, groups, chunks, chunk_rows, model), BF16),
             pltpu.VMEM((tokens, tokens), F32),
             dma((2,)), dma((heads,)), dma((heads,)), dma((SLOTS, 3)), dma((2,)), dma((2,)),
-            dma((chunks, groups - 1)), dma((chunks, groups)), dma((chunks, 2 * groups - 1)), dma((chunks, 2, groups)),
+            dma((chunks, groups - 1)), dma((chunks, groups)), dma((chunks, 2 * groups - 1)), dma((chunks, 2, groups)), dma((4,)),
         ],
-        compiler_params=pltpu.CompilerParams(vmem_limit_bytes=VMEM_LIMIT, collective_id=1, has_side_effects=True),
+        compiler_params=pltpu.CompilerParams(vmem_limit_bytes=58 * MIB, collective_id=1, has_side_effects=True),
         name="last",
-    )(h, part, mask, idx, scale, router, w_query, w_out, keys, values, exp_gate, exp_up, exp_down)
+    )(pltpu.with_memory_space_constraint(h, pltpu.VMEM), pltpu.with_memory_space_constraint(part, pltpu.VMEM), *map(pinned, (mask, idx, scale, router, w_query, w_out, keys, values, exp_gate, exp_up, exp_down)))
 
 
 def decode_body(groups, hidden, write_pos, enc_mask, expert_idx, self_keys, self_values, cross_keys, cross_values, rel_bias, norm_scale, w_query, w_key, w_value, w_out, w_cross_query, w_cross_out, dense_gate, dense_up, dense_down, router, exp_gate, exp_up, exp_down):
@@ -555,9 +620,10 @@
     mask = jnp.transpose(enc_mask)
     scale = jnp.transpose(norm_scale, (1, 0, 2))
     keys, values, ckeys, cvalues = map(lanes, (self_keys, self_values, cross_keys, cross_values))
-    part, bias, k_out, v_out = self_attention(0, hidden, pos, scale, rel_bias, w_query, w_key, w_value, w_out, keys, values)
-    h = middle(0, hidden, part, mask, scale, w_cross_query, w_cross_out, ckeys, cvalues, dense_gate, dense_up, dense_down)
-    part, k_out, v_out = self_attention(1, h, pos, scale, bias, w_query, w_key, w_value, w_out, keys, values, (k_out, v_out))
+    part, bias, k_out, v_out = self_first(0, hidden, pos, scale, rel_bias, w_query, w_key, w_value, w_out, keys, values)
+    following = (w_query, w_key, w_value, w_out, keys, values)
+    h, pos, scale_in, w_in, w_o, keys, values = middle(0, part, hidden, mask, scale, pos, w_cross_query, w_cross_out, ckeys, cvalues, dense_gate, dense_up, dense_down, following)
+    part, k_out, v_out = self_second(1, h, pos, scale_in, bias, w_in, w_o, keys, values, k_out, v_out)
     h = last(1, h, part, mask, idx, scale, jnp.transpose(router), w_cross_query, w_cross_out, ckeys, cvalues, exp_gate, exp_up, exp_down, groups)
     return h, jnp.transpose(k_out, (0, 4, 1, 2, 3)), jnp.transpose(v_out, (0, 4, 1, 2, 3))
 

time: 101 us -> 85.1 us (0.84)
  Pallas kernels: 98.8 us -> 83.7 us
    pallas_call x4, Pallas kernels: 98.8 us -> 83.7 us  [the longest x1 50.5 us: last(): pl.pallas_call(functools.partial(last_kernel, layer), out_shape=pltpu.VME...]
where the time goes in v2:
time: 85.1 us; the launch traced here: 85 us
  Pallas kernels  83.7 us (98%)
    pallas_call x1, Pallas kernels, last(): pl.pallas_call(functools.partial(last_kernel, layer), out_shape=pltpu.VME...  50.5 us
    pallas_call x1, Pallas kernels, middle(): pl.pallas_call(functools.partial(middle_kernel, layer), out_shape=[pltpu....  22.9 us
    pallas_call x1, Pallas kernels, self_first(): pl.pallas_call(functools.partial(first_kernel, layer), out_shape=[pltpu.V...  6.46 us
    pallas_call x1, Pallas kernels, self_second(): pl.pallas_call(functools.partial(second_kernel, layer), out_shape=[pltpu....  3.85 us

profile of v2, /device:TPU:0, one launch (start us, length us, event | category | flops | bytes accessed | tf_op | source)
XLA Modules:
  0.0 85.0 jit_solution(17738684427597208880)
XLA Ops:
  0.6 6.5 %self_first.1 = (bf16[128,768]{1,0:T(8,128)(2,1)S(1)}, f32[6,32,128]{2,1,0:T(8,128)S(1)}, bf16[2,6,32,64,128]{4,3,2,1,0:T(8,128)(2,1)}, bf16[2,6,32,64,128]{4,3,2,1,0:T(8,128)(2,1)}) custom-call(bf16[128,768]{1,0:T(8,128)(2,1)} %h_hbm.3, s32[1,128]{1,0:T(1,128)} %bitcast.27, f32[3,2,768]{2,1,0:T(2,128)} %bitcast.22, f32[6,32]{1,0:T(8,128)} %rel_hbm.1, ...), custom_call_target="tpu_custom_call" | custom-call | tf_op jit(solution)/shard_map/self_first/pallas_call | solution.py:205
  7.1 22.9 %middle.1 = (bf16[128,768]{1,0:T(8,128)(2,1)S(1)}, s32[1,128]{1,0:T(1,128)S(1)}, f32[3,2,768]{2,1,0:T(2,128)S(1)}, bf16[3,768,384]{2,1,0:T(8,128)(2,1)S(1)}, bf1...) custom-call(bf16[128,768]{1,0:T(8,128)(2,1)S(1)} %get-tuple-element.17.part_ref, ...), custom_call_target="tpu_custom_call" | custom-call | tf_op jit(solution)/shard_map/middle/pallas_call | solution.py:356
  30.0 3.8 %self_second.1 = (bf16[128,768]{1,0:T(8,128)(2,1)S(1)}, bf16[2,6,32,64,128]{4,3,2,1,0:T(8,128)(2,1)}, bf16[2,6,32,64,128]{4,3,2,1,0:T(8,128)(2,1)}) custom-call(bf16[128,768]{1,0:T(8,128)(2,1)S(1)} %get-tuple-element.18.h_ref, s32[1,128]{1,0:T(1,128)S(1)} %get-tuple-element.19.pos_ref, ...), custom_call_target="tpu_custom_call", output_to_operand_aliasing={{1}: (8, {}), {2}: (9, {})} | custom-call | tf_op jit(solution)/shard_map/self_second/pallas_call | solution.py:231
  33.9 50.5 %last.1 = bf16[128,768]{1,0:T(8,128)(2,1)S(1)} custom-call(bf16[128,768]{1,0:T(8,128)(2,1)S(1)} %get-tuple-element.18.h_ref, bf16[128,768]{1,0:T(8,128)(2,1)S(1)} %get-tuple-element.28.part_ref, s32[32,128]{1,0:T(8,128)} %bitcast.26, s32[1,128]{1,0:T(1,128)} %bitcast.29, f32[3,2,768]{2,1,0:T(2,128)} %bitcast.24, f32[64,768]{1,0:T(8,128)} %bitcast.21, ...), custom_call_target="tpu_custom_call" | custom-call | tf_op jit(solution)/shard_map/last/pallas_call | solution.py:575
  84.4 0.7 copy.31

commit v3 on v2

--- a/solution.py
+++ b/solution.py
@@ -13,7 +13,9 @@
 BF16 = jnp.bfloat16
 F32 = jnp.float32
 MIB = 1024 * 1024
-SLOTS = 6
+GATE_SLOTS = 7
+DOWN_SLOTS = 7
+LAST_VMEM = 62 * MIB
 
 
 def rms_norm(h_float, scale):
@@ -388,36 +390,40 @@
 def last_kernel(layer, h_ref, part_ref, mask_hbm, idx_hbm, scale_hbm, router_hbm, wq_hbm, wo_hbm, k_hbm, v_hbm, eg_hbm, eu_hbm, ed_hbm,
                 out_ref,
                 mask_ref, idx_ref, scale_ref, router_ref, wq_ref, wo_ref, keys, values, eg_ref, eu_ref, ed_ref, q_t, acc_ref, p_ref, ctx_t, mine_ref, other_ref,
-                place_ref, send_x, recv_x, rows_ref, y_ref, send_y, recv_y, gate_ref,
-                w_sem, k_sem, v_sem, e_sem, tp_send, tp_recv, x_send, x_recv, y_send, y_recv, s_sem):
-    heads = keys.shape[0]
+                place_ref, send_x, recv_x, product_ref, send_y, recv_y, comb_ref, gate_ref,
+                w_sem, k_sem, v_sem, g_sem, d_sem, tp_send, tp_recv, x_send, x_recv, y_send, y_recv, s_sem):
+    heads = k_sem.shape[0]
     tokens, model = h_ref.shape
     experts = router_ref.shape[0]
+    local, groups, capacity, _ = recv_x.shape
+    rows = groups * capacity
+    g_slots, d_slots = eg_ref.shape[0], ed_ref.shape[0]
+    tp = lax.axis_index("tp")
+    ep = lax.axis_index("ep")
+    me = tp * groups + ep
+
+    def peer_ep(offset):
+        return lax.rem(ep + offset, groups)
+
+    def peer_tp(offset):
+        return lax.rem(tp + offset, 2)
+
+    def k_in(head):
+        return pltpu.make_async_copy(k_hbm.at[layer, head], keys.at[head], k_sem.at[head])
+
+    def v_in(head):
+        return pltpu.make_async_copy(v_hbm.at[layer, head], values.at[head], v_sem.at[head])
+
+    def gate_up_in(expert):
+        slot = lax.rem(expert, g_slots)
+        return [pltpu.make_async_copy(s.at[expert], d.at[slot], g_sem.at[slot, i]) for i, (s, d) in enumerate(((eg_hbm, eg_ref), (eu_hbm, eu_ref)))]
+
+    def down_in(expert):
+        slot = lax.rem(expert, d_slots)
+        return pltpu.make_async_copy(ed_hbm.at[expert], ed_ref.at[slot], d_sem.at[slot])
+
     small = [pltpu.make_async_copy(s, d, s_sem.at[i]) for i, (s, d) in enumerate(
         ((mask_hbm, mask_ref), (idx_hbm, idx_ref), (scale_hbm, scale_ref), (router_hbm, router_ref)))]
-    groups, chunks, chunk_rows, _ = recv_x.shape
-    local = experts // groups
-    capacity = place_ref.shape[0] // experts
-    per_chunk = local // chunks
-    tp = lax.axis_index("tp")
-    ep = lax.axis_index("ep")
-
-    def peer_ep(offset):
-        return lax.rem(ep + offset, groups)
-
-    def peer_tp(offset):
-        return lax.rem(tp + offset, 2)
-
-    def k_in(head):
-        return pltpu.make_async_copy(k_hbm.at[layer, head], keys.at[head], k_sem.at[head])
-
-    def v_in(head):
-        return pltpu.make_async_copy(v_hbm.at[layer, head], values.at[head], v_sem.at[head])
-
-    def weights_in(expert, slot):
-        return [pltpu.make_async_copy(s.at[expert], d.at[slot], e_sem.at[slot, i])
-                for i, (s, d) in enumerate(((eg_hbm, eg_ref), (eu_hbm, eu_ref), (ed_hbm, ed_ref)))]
-
     wq_copy = pltpu.make_async_copy(wq_hbm.at[layer], wq_ref, w_sem.at[0])
     wo_copy = pltpu.make_async_copy(wo_hbm.at[layer], wo_ref, w_sem.at[1])
 
@@ -433,8 +439,8 @@
     for head in range(heads):
         v_in(head).start()
     wo_copy.start()
-    for slot in range(SLOTS):
-        for c in weights_in(slot, slot):
+    for expert in range(max(g_slots, d_slots)):
+        for c in (gate_up_in(expert) if expert < g_slots else []) + ([down_in(expert)] if expert < d_slots else []):
             c.start(priority=1)
     pl.semaphore_wait(barrier, len(others))
 
@@ -448,7 +454,7 @@
     earlier = (lax.broadcasted_iota(jnp.int32, (tokens, tokens), 0) < lax.broadcasted_iota(jnp.int32, (tokens, tokens), 1)).astype(F32)
     counts = dot(onehot.astype(BF16), earlier.astype(BF16))
     slot_of = jnp.sum(counts * onehot, axis=0, keepdims=True).astype(jnp.int32)
-    row_of = jnp.where(slot_of < capacity, idx * capacity + slot_of, -1)
+    row_of = jnp.where(slot_of < capacity, lax.rem(idx, local) * rows + lax.div(idx, local) * capacity + slot_of, -1)
     place_ref[...] = (lax.broadcasted_iota(jnp.int32, (experts * capacity, tokens), 0) == row_of).astype(F32).astype(BF16)
 
     copies[0].wait()
@@ -460,24 +466,39 @@
     h_float = add_parts(h_float, mine_ref[...], other_ref[1])
     x = rms_norm(h_float, scale_ref[2, layer:layer + 1, :])
 
-    send_x[...] = dot(place_ref[...], x).astype(BF16).reshape(send_x.shape)
-
-    def x_copy(chunk, offset):
+    def x_copy(expert, offset):
         return pltpu.make_async_remote_copy(
-            src_ref=send_x.at[peer_ep(offset), chunk], dst_ref=recv_x.at[ep, chunk],
-            send_sem=x_send.at[chunk, offset - 1], recv_sem=x_recv.at[chunk, ep],
+            src_ref=send_x.at[expert, peer_ep(offset)], dst_ref=recv_x.at[expert, ep],
+            send_sem=x_send.at[expert], recv_sem=x_recv.at[expert],
             device_id={"ep": peer_ep(offset)}, device_id_type=MESH)
 
-    def x_arrival(chunk, offset):
+    def x_all(expert):
         return pltpu.make_async_remote_copy(
-            src_ref=send_x.at[peer_ep(offset), chunk], dst_ref=recv_x.at[peer_ep(offset), chunk],
-            send_sem=x_send.at[chunk, offset - 1], recv_sem=x_recv.at[chunk, peer_ep(offset)],
-            device_id={"ep": peer_ep(offset)}, device_id_type=MESH)
-
-    for chunk in range(chunks):
+            src_ref=send_x.at[expert, 0:groups - 1], dst_ref=recv_x.at[expert, 0:groups - 1],
+            send_sem=x_send.at[expert], recv_sem=x_recv.at[expert],
+            device_id={"ep": peer_ep(1)}, device_id_type=MESH)
+
+    def y_copy(expert, number):
+        dt, de = others[number]
+        return pltpu.make_async_remote_copy(
+            src_ref=send_y.at[expert, peer_ep(de)], dst_ref=recv_y.at[expert, me],
+            send_sem=y_send.at[expert], recv_sem=y_recv.at[expert],
+            device_id={"tp": peer_tp(dt), "ep": peer_ep(de)}, device_id_type=MESH)
+
+    def y_all(expert):
+        return pltpu.make_async_remote_copy(
+            src_ref=recv_y.at[expert, 0:2 * groups - 1], dst_ref=recv_y.at[expert, 0:2 * groups - 1],
+            send_sem=y_send.at[expert], recv_sem=y_recv.at[expert],
+            device_id={"ep": peer_ep(1)}, device_id_type=MESH)
+
+    buffers = dot(place_ref[...], x).astype(BF16)
+    for expert in range(local):
+        for g in range(groups):
+            first = expert * rows + g * capacity
+            send_x[expert, g] = buffers[first:first + capacity]
         for offset in range(1, groups):
-            x_copy(chunk, offset).start()
-    recv_x[ep] = send_x[ep]
+            x_copy(expert, offset).start()
+    recv_x[:, ep] = send_x[:, ep]
 
     router = router_ref[...]
     high = router.astype(BF16)
@@ -489,76 +510,69 @@
     gate = jnp.sum(logits_exp * onehot, axis=0, keepdims=True) / jnp.sum(logits_exp, axis=0, keepdims=True)
     gate_ref[...] = jnp.transpose(jnp.broadcast_to(gate, (tokens, tokens)))
 
-    block = groups * chunk_rows
-    r0 = lax.broadcasted_iota(jnp.int32, (block, block), 0)
-    r1 = lax.broadcasted_iota(jnp.int32, (block, block), 1)
-    group_rows = groups * capacity
-    source = ((r0 % group_rows) // capacity) * chunk_rows + (r0 // group_rows) * capacity + r0 % capacity
-    to_experts = (r1 == source).astype(F32).astype(BF16)
-    back = ((r0 % chunk_rows) // capacity) * group_rows + (r0 // chunk_rows) * capacity + r0 % capacity
-    to_groups = (r1 == back).astype(F32).astype(BF16)
-
-    def y_copy(chunk, number):
-        dt, de = others[number]
-        return pltpu.make_async_remote_copy(
-            src_ref=send_y.at[chunk, peer_ep(de)], dst_ref=recv_y.at[tp, ep, chunk],
-            send_sem=y_send.at[chunk, number], recv_sem=y_recv.at[chunk, tp, ep],
-            device_id={"tp": peer_tp(dt), "ep": peer_ep(de)}, device_id_type=MESH)
-
-    def y_arrival(chunk, number):
-        dt, de = others[number]
-        return pltpu.make_async_remote_copy(
-            src_ref=send_y.at[chunk, peer_ep(de)], dst_ref=recv_y.at[peer_tp(dt), peer_ep(de), chunk],
-            send_sem=y_send.at[chunk, number], recv_sem=y_recv.at[chunk, peer_tp(dt), peer_ep(de)],
-            device_id={"tp": peer_tp(dt), "ep": peer_ep(de)}, device_id_type=MESH)
+    def gate_up(expert):
+        slot = lax.rem(expert, g_slots)
+        x_rows = jnp.concatenate([recv_x[expert, g].astype(F32) for g in range(groups)], axis=0).astype(BF16)
+        return (jax.nn.gelu(dot(x_rows, eg_ref[slot])) * dot(x_rows, eu_ref[slot])).astype(BF16)
+
+    def send_result(expert, y):
+        for g in range(groups):
+            send_y[expert, g] = y[g * capacity:(g + 1) * capacity]
+        for number in range(len(others)):
+            y_copy(expert, number).start()
+        recv_y[expert, me] = send_y[expert, ep]
+
+    def wait_gate_up(expert):
+        x_all(expert).wait_recv()
+        for c in gate_up_in(expert):
+            c.wait()
+
+    def collect(expert):
+        y_all(expert).wait_recv()
+        blocks = [recv_y[expert, g].astype(F32) + recv_y[expert, groups + g].astype(F32) for g in range(groups)]
+        comb_ref[pl.ds(pl.multiple_of(expert * rows, rows), rows), :] = jnp.concatenate(blocks, axis=0).astype(BF16)
+
+    wait_gate_up(0)
+    product_ref[0] = gate_up(0)
+    for c in gate_up_in(g_slots):
+        c.start(priority=1)
+    lag = 4
 
     def expert_step(expert, carry):
-        slot = lax.rem(expert, SLOTS)
-        first_row = pl.multiple_of(lax.rem(expert, per_chunk) * group_rows, group_rows)
-        rows = rows_ref[pl.ds(first_row, group_rows), :]
-        w_copies = weights_in(expert, slot)
-        w_copies[0].wait()
-        gate_in = dot(rows, eg_ref[slot])
-        w_copies[1].wait()
-        lin_in = dot(rows, eu_ref[slot])
-        product = (jax.nn.gelu(gate_in) * lin_in).astype(BF16)
-        w_copies[2].wait()
-        y_ref[pl.ds(first_row, group_rows), :] = dot(product, ed_ref[slot]).astype(BF16)
-
-        @pl.when(expert + SLOTS < local)
+        wait_gate_up(expert)
+        down_in(expert - 1).wait()
+        before = product_ref[lax.rem(expert - 1, 2)]
+        y = dot(before, ed_ref[lax.rem(expert - 1, d_slots)]).astype(BF16)
+        product_ref[lax.rem(expert, 2)] = gate_up(expert)
+        send_result(expert - 1, y)
+
+        @pl.when(expert + g_slots < local)
         def _():
-            for c in weights_in(expert + SLOTS, slot):
+            for c in gate_up_in(expert + g_slots):
                 c.start(priority=1)
+
+        @pl.when(expert - 1 + d_slots < local)
+        def _():
+            down_in(expert - 1 + d_slots).start(priority=1)
+
+        @pl.when(expert >= lag)
+        def _():
+            collect(expert - lag)
         return carry
 
-    def chunk_step(chunk, carry):
-        for offset in range(1, groups):
-            x_arrival(chunk, offset).wait_recv()
-        arrived = recv_x[:, chunk].reshape(block, model)
-        rows_ref[...] = dot(to_experts, arrived).astype(BF16)
-        lax.fori_loop(chunk * per_chunk, (chunk + 1) * per_chunk, expert_step, 0)
-        send_y[chunk] = dot(to_groups, y_ref[...]).astype(BF16).reshape(groups, chunk_rows, model)
-        for number in range(len(others)):
-            y_copy(chunk, number).start()
-        recv_y[tp, ep, chunk] = send_y[chunk, ep]
-        return carry
-
-    lax.fori_loop(0, chunks, chunk_step, 0)
-
-    for chunk in range(chunks):
-        for number in range(len(others)):
-            y_arrival(chunk, number).wait_recv()
-    returned = (recv_y[0].astype(F32) + recv_y[1].astype(F32)).astype(BF16).reshape(experts * capacity, model)
-    combined = dot_t(place_ref[...], returned)
+    lax.fori_loop(1, local, expert_step, 0)
+    down_in(local - 1).wait()
+    send_result(local - 1, dot(product_ref[(local - 1) % 2], ed_ref[(local - 1) % d_slots]).astype(BF16))
+    for expert in range(local - lag, local):
+        collect(expert)
+    combined = dot_t(place_ref[...], comb_ref[...])
     gate_col = gate_ref[...]
     for c in range(0, model, tokens):
         delta = gate_col * combined[:, c:c + tokens]
         out_ref[:, c:c + tokens] = (h_float[:, c:c + tokens] + delta).astype(BF16)
-    for chunk in range(chunks):
-        for offset in range(1, groups):
-            x_copy(chunk, offset).wait_send()
-        for number in range(len(others)):
-            y_copy(chunk, number).wait_send()
+    for expert in range(local):
+        x_all(expert).wait_send()
+        y_all(expert).wait_send()
 
 
 def last(layer, h, part, mask, idx, scale, router, w_query, w_out, keys, values, exp_gate, exp_up, exp_down, groups):
@@ -567,11 +581,10 @@
     local, _, ff = exp_gate.shape
     experts = router.shape[0]
     capacity = (2 * tokens + experts - 1) // experts
-    chunk_rows = 16
-    chunks = local * capacity // chunk_rows
     vmem = pl.BlockSpec(memory_space=pltpu.VMEM)
     hbm = pl.BlockSpec(memory_space=pltpu.HBM)
     dma = pltpu.SemaphoreType.DMA
+    on_chip = functools.partial(pltpu.with_memory_space_constraint, memory_space=pltpu.VMEM)
     return pl.pallas_call(
         functools.partial(last_kernel, layer),
         out_shape=pltpu.VMEM((tokens, model), BF16),
@@ -586,9 +599,9 @@
             pltpu.VMEM((width, model), BF16),
             pltpu.VMEM((heads, slots, head_dim, tokens), BF16),
             pltpu.VMEM((heads, slots, head_dim, tokens), BF16),
-            pltpu.VMEM((SLOTS, model, ff), BF16),
-            pltpu.VMEM((SLOTS, model, ff), BF16),
-            pltpu.VMEM((SLOTS, ff, model), BF16),
+            pltpu.VMEM((GATE_SLOTS, model, ff), BF16),
+            pltpu.VMEM((GATE_SLOTS, model, ff), BF16),
+            pltpu.VMEM((DOWN_SLOTS, ff, model), BF16),
             pltpu.VMEM((heads, head_dim, tokens), F32),
             pltpu.VMEM((heads, slots * 8, tokens), F32),
             pltpu.VMEM((heads, slots, tokens), F32),
@@ -596,19 +609,19 @@
             pltpu.VMEM((tokens, model), BF16),
             pltpu.VMEM((2, tokens, model), BF16),
             pltpu.VMEM((experts * capacity, tokens), BF16),
-            pltpu.VMEM((groups, chunks, chunk_rows, model), BF16),
-            pltpu.VMEM((groups, chunks, chunk_rows, model), BF16),
-            pltpu.VMEM((groups * chunk_rows, model), BF16),
-            pltpu.VMEM((groups * chunk_rows, model), BF16),
-            pltpu.VMEM((chunks, groups, chunk_rows, model), BF16),
-            pltpu.VMEM((2, groups, chunks, chunk_rows, model), BF16),
+            pltpu.VMEM((local, groups, capacity, model), BF16),
+            pltpu.VMEM((local, groups, capacity, model), BF16),
+            pltpu.VMEM((2, groups * capacity, ff), BF16),
+            pltpu.VMEM((local, groups, capacity, model), BF16),
+            pltpu.VMEM((local, 2 * groups, capacity, model), BF16),
+            pltpu.VMEM((experts * capacity, model), BF16),
             pltpu.VMEM((tokens, tokens), F32),
-            dma((2,)), dma((heads,)), dma((heads,)), dma((SLOTS, 3)), dma((2,)), dma((2,)),
-            dma((chunks, groups - 1)), dma((chunks, groups)), dma((chunks, 2 * groups - 1)), dma((chunks, 2, groups)), dma((4,)),
+            dma((2,)), dma((heads,)), dma((heads,)), dma((GATE_SLOTS, 2)), dma((DOWN_SLOTS,)), dma((2,)), dma((2,)),
+            dma((local,)), dma((local,)), dma((local,)), dma((local,)), dma((4,)),
         ],
-        compiler_params=pltpu.CompilerParams(vmem_limit_bytes=58 * MIB, collective_id=1, has_side_effects=True),
+        compiler_params=pltpu.CompilerParams(vmem_limit_bytes=LAST_VMEM, collective_id=1, has_side_effects=True),
         name="last",
-    )(pltpu.with_memory_space_constraint(h, pltpu.VMEM), pltpu.with_memory_space_constraint(part, pltpu.VMEM), *map(pinned, (mask, idx, scale, router, w_query, w_out, keys, values, exp_gate, exp_up, exp_down)))
+    )(on_chip(h), on_chip(part), *map(pinned, (mask, idx, scale, router, w_query, w_out, keys, values, exp_gate, exp_up, exp_down)))
 
 
 def decode_body(groups, hidden, write_pos, enc_mask, expert_idx, self_keys, self_values, cross_keys, cross_values, rel_bias, norm_scale, w_query, w_key, w_value, w_out, w_cross_query, w_cross_out, dense_gate, dense_up, dense_down, router, exp_gate, exp_up, exp_down):

time: 85.1 us -> 79.2 us (0.931)
  Pallas kernels: 83.7 us -> 77.7 us
    pallas_call x1, Pallas kernels: 50.5 us -> 44.5 us  [last(): pl.pallas_call(functools.partial(last_kernel, layer), out_shape=pltpu.VME...]
where the time goes in v3:
time: 79.2 us; the launch traced here: 79.1 us
  Pallas kernels  77.7 us (98%)
    pallas_call x1, Pallas kernels, last(): pl.pallas_call(functools.partial(last_kernel, layer), out_shape=pltpu.VME...  44.5 us
    pallas_call x1, Pallas kernels, middle(): pl.pallas_call(functools.partial(middle_kernel, layer), out_shape=[pltpu....  22.9 us
    pallas_call x1, Pallas kernels, self_first(): pl.pallas_call(functools.partial(first_kernel, layer), out_shape=[pltpu.V...  6.46 us
    pallas_call x1, Pallas kernels, self_second(): pl.pallas_call(functools.partial(second_kernel, layer), out_shape=[pltpu....  3.85 us

profile of v3, /device:TPU:0, one launch (start us, length us, event | category | flops | bytes accessed | tf_op | source)
XLA Modules:
  0.0 79.1 jit_solution(11973681281757925205)
XLA Ops:
  0.6 6.5 %self_first.1 = (bf16[128,768]{1,0:T(8,128)(2,1)S(1)}, f32[6,32,128]{2,1,0:T(8,128)S(1)}, bf16[2,6,32,64,128]{4,3,2,1,0:T(8,128)(2,1)}, bf16[2,6,32,64,128]{4,3,2,1,0:T(8,128)(2,1)}) custom-call(bf16[128,768]{1,0:T(8,128)(2,1)} %h_hbm.3, s32[1,128]{1,0:T(1,128)} %bitcast.27, f32[3,2,768]{2,1,0:T(2,128)} %bitcast.22, f32[6,32]{1,0:T(8,128)} %rel_hbm.1, ...), custom_call_target="tpu_custom_call" | custom-call | tf_op jit(solution)/shard_map/self_first/pallas_call | solution.py:207
  7.1 22.9 %middle.1 = (bf16[128,768]{1,0:T(8,128)(2,1)S(1)}, s32[1,128]{1,0:T(1,128)S(1)}, f32[3,2,768]{2,1,0:T(2,128)S(1)}, bf16[3,768,384]{2,1,0:T(8,128)(2,1)S(1)}, bf1...) custom-call(bf16[128,768]{1,0:T(8,128)(2,1)S(1)} %get-tuple-element.17.part_ref, ...), custom_call_target="tpu_custom_call" | custom-call | tf_op jit(solution)/shard_map/middle/pallas_call | solution.py:358
  30.0 3.8 %self_second.1 = (bf16[128,768]{1,0:T(8,128)(2,1)S(1)}, bf16[2,6,32,64,128]{4,3,2,1,0:T(8,128)(2,1)}, bf16[2,6,32,64,128]{4,3,2,1,0:T(8,128)(2,1)}) custom-call(bf16[128,768]{1,0:T(8,128)(2,1)S(1)} %get-tuple-element.18.h_ref, s32[1,128]{1,0:T(1,128)S(1)} %get-tuple-element.19.pos_ref, ...), custom_call_target="tpu_custom_call", output_to_operand_aliasing={{1}: (8, {}), {2}: (9, {})} | custom-call | tf_op jit(solution)/shard_map/self_second/pallas_call | solution.py:233
  33.9 44.5 %last.1 = bf16[128,768]{1,0:T(8,128)(2,1)S(1)} custom-call(bf16[128,768]{1,0:T(8,128)(2,1)S(1)} %get-tuple-element.18.h_ref, bf16[128,768]{1,0:T(8,128)(2,1)S(1)} %get-tuple-element.28.part_ref, s32[32,128]{1,0:T(8,128)} %bitcast.26, s32[1,128]{1,0:T(1,128)} %bitcast.29, f32[3,2,768]{2,1,0:T(2,128)} %bitcast.24, f32[64,768]{1,0:T(8,128)} %bitcast.21, ...), custom_call_target="tpu_custom_call" | custom-call | tf_op jit(solution)/shard_map/last/pallas_call | solution.py:588
  78.4 0.7 copy.31

commit v4 on v3

--- a/solution.py
+++ b/solution.py
@@ -13,8 +13,8 @@
 BF16 = jnp.bfloat16
 F32 = jnp.float32
 MIB = 1024 * 1024
-GATE_SLOTS = 7
-DOWN_SLOTS = 7
+GATE_SLOTS = 8
+DOWN_SLOTS = 8
 LAST_VMEM = 62 * MIB
 
 
@@ -43,8 +43,8 @@
 
 
 def score_head(q_head, keys, head, acc_ref, merge=None):
-    for slot in range(keys.shape[1]):
-        k_slot = keys[head, slot]
+    for slot in range(acc_ref.shape[1] // 8):
+        k_slot = keys(head, slot) if callable(keys) else keys[head, slot]
         if merge is not None:
             pos_b, k_new, merged = merge
             k_slot = jnp.where(pos_b == jnp.asarray(slot, BF16), k_new, k_slot)
@@ -67,8 +67,8 @@
 
 def context_head(p_ref, values, head, merge=None):
     total = None
-    for slot in range(values.shape[1]):
-        v_slot = values[head, slot]
+    for slot in range(p_ref.shape[1]):
+        v_slot = values(head, slot) if callable(values) else values[head, slot]
         if merge is not None:
             pos_b, v_new, merged = merge
             v_slot = jnp.where(pos_b == jnp.asarray(slot, BF16), v_new, v_slot)
@@ -83,9 +83,9 @@
 
 
 def first_kernel(layer, h_hbm, pos_hbm, scale_hbm, rel_hbm, wq_hbm, wk_hbm, wv_hbm, wo_hbm, k_hbm, v_hbm,
-                 part_ref, bias_ref, ko_hbm, vo_hbm,
-                 h_ref, pos_ref, scale_ref, rel_ref, w_in, wo_ref, keys, values, q_t, k_t, v_t, acc_ref, p_ref, ctx_t,
-                 s_sem, w_sem, k_sem, v_sem, ko_sem, vo_sem):
+                 part_ref, bias_ref, ko_hbm, values,
+                 h_ref, pos_ref, scale_ref, rel_ref, w_in, wo_ref, keys, q_t, k_t, v_t, acc_ref, p_ref, ctx_t,
+                 s_sem, w_sem, k_sem, v_sem, ko_sem):
     heads = keys.shape[0]
     small = [pltpu.make_async_copy(s, d, s_sem.at[i]) for i, (s, d) in enumerate(
         ((h_hbm, h_ref), (scale_hbm, scale_ref), (pos_hbm, pos_ref), (rel_hbm, rel_ref)))]
@@ -121,15 +121,18 @@
 
     self_part(layer, h_ref, pos_ref, scale_ref, bias_ref, w_in, [c.wait for c in w_copies], wo_ref, wo_copy.wait,
               keys, values, lambda head: k_in(head).wait(), lambda head: v_in(head).wait(), keys, values,
-              part_ref, ko_hbm, vo_hbm, q_t, k_t, v_t, acc_ref, p_ref, ctx_t, ko_sem, vo_sem)
-
-
-def second_kernel(layer, h_ref, pos_ref, scale_ref, bias_ref, w_in, wo_ref, keys_in, values_in, _, __,
+              part_ref, ko_hbm, None, q_t, k_t, v_t, acc_ref, p_ref, ctx_t, ko_sem, None)
+
+
+def second_kernel(layer, h_ref, pos_ref, scale_ref, bias_ref, w_in, wo_ref, keys_in, values_in, values_before, _,
                   part_ref, ko_hbm, vo_hbm,
-                  keys, values, q_t, k_t, v_t, acc_ref, p_ref, ctx_t, ko_sem, vo_sem):
+                  keys, values, q_t, k_t, v_t, acc_ref, p_ref, ctx_t, ko_sem, vo_sem, before_sem):
+    before = pltpu.make_async_copy(values_before, vo_hbm.at[layer - 1], before_sem)
+    before.start()
     self_part(layer, h_ref, pos_ref, scale_ref, bias_ref, w_in, [None] * 3, wo_ref, None,
               keys_in, values_in, None, None, keys, values,
               part_ref, ko_hbm, vo_hbm, q_t, k_t, v_t, acc_ref, p_ref, ctx_t, ko_sem, vo_sem)
+    before.wait()
 
 
 def self_part(layer, h_ref, pos_ref, scale_ref, bias_ref, w_in, w_waits, wo_ref, wo_wait,
@@ -170,7 +173,8 @@
         if v_wait is not None:
             v_wait(head)
         ctx_t[head] = context_head(p_ref, values_in, head, (pos_b, v_t[head], values))
-        v_out(head).start()
+        if vo_hbm is not None:
+            v_out(head).start()
         return carry
 
     lax.fori_loop(0, heads, context_step, 0)
@@ -180,7 +184,8 @@
     part_ref[...] = dot(ctx, wo_ref[...]).astype(BF16)
     for head in range(heads):
         k_out(head).wait()
-        v_out(head).wait()
+        if vo_hbm is not None:
+            v_out(head).wait()
 
 
 def attention_scratch(heads, slots, head_dim, tokens):
@@ -206,9 +211,12 @@
     cache = pltpu.HBM(keys.shape, keys.dtype)
     return pl.pallas_call(
         functools.partial(first_kernel, layer),
-        out_shape=[pltpu.VMEM((tokens, model), BF16), pltpu.VMEM((heads, slots, tokens), F32), cache, cache],
+        out_shape=[
+            pltpu.VMEM((tokens, model), BF16), pltpu.VMEM((heads, slots, tokens), F32), cache,
+            pltpu.VMEM((heads, slots, head_dim, tokens), BF16),
+        ],
         in_specs=[hbm] * 10,
-        out_specs=[vmem, vmem, hbm, hbm],
+        out_specs=[vmem, vmem, hbm, vmem],
         scratch_shapes=[
             pltpu.VMEM((tokens, model), BF16),
             pltpu.VMEM(pos.shape, pos.dtype),
@@ -216,15 +224,15 @@
             pltpu.SMEM(rel.shape, F32),
             pltpu.VMEM((3, model, width), BF16),
             pltpu.VMEM((width, model), BF16),
-        ] + attention_scratch(heads, slots, head_dim, tokens) + [
-            dma((4,)), dma((4,)), dma((heads,)), dma((heads,)), dma((heads,)), dma((heads,)),
+        ] + attention_scratch(heads, slots, head_dim, tokens)[1:] + [
+            dma((4,)), dma((4,)), dma((heads,)), dma((heads,)), dma((heads,)),
         ],
         compiler_params=pltpu.CompilerParams(vmem_limit_bytes=20 * MIB),
         name="self_first",
     )(*ins)
 
 
-def self_second(layer, h, pos, scale, bias, w_in, w_out, keys_in, values_in, k_out, v_out):
+def self_second(layer, h, pos, scale, bias, w_in, w_out, keys_in, values_in, values_before, k_out):
     heads, slots, head_dim, tokens = keys_in.shape
     vmem = pl.BlockSpec(memory_space=pltpu.VMEM)
     hbm = pl.BlockSpec(memory_space=pltpu.HBM)
@@ -233,19 +241,41 @@
     return pl.pallas_call(
         functools.partial(second_kernel, layer),
         out_shape=[pltpu.VMEM(h.shape, BF16), cache, cache],
-        in_specs=[vmem] * 8 + [hbm] * 2,
+        in_specs=[vmem] * 9 + [hbm],
         out_specs=[vmem, hbm, hbm],
-        input_output_aliases={8: 1, 9: 2},
-        scratch_shapes=attention_scratch(heads, slots, head_dim, tokens) + [dma((heads,)), dma((heads,))],
+        input_output_aliases={9: 1},
+        scratch_shapes=attention_scratch(heads, slots, head_dim, tokens) + [dma((heads,)), dma((heads,)), dma],
         compiler_params=pltpu.CompilerParams(vmem_limit_bytes=20 * MIB),
         name="self_second",
-    )(h, pos, scale, bias, w_in, w_out, keys_in, values_in, pinned(k_out), pinned(v_out))
+    )(h, pos, scale, bias, w_in, w_out, keys_in, values_in, values_before, pinned(k_out))
 
 
 def tp_exchange(src, dst, send_sem, recv_sem):
-    return pltpu.make_async_remote_copy(
-        src_ref=src, dst_ref=dst, send_sem=send_sem, recv_sem=recv_sem,
-        device_id={"tp": 1 - lax.axis_index("tp")}, device_id_type=MESH)
+    rows = src.shape[0] // 2
+    return [pltpu.make_async_remote_copy(
+        src_ref=src.at[i * rows:(i + 1) * rows], dst_ref=dst.at[i * rows:(i + 1) * rows],
+        send_sem=send_sem.at[i], recv_sem=recv_sem.at[i],
+        device_id={"tp": 1 - lax.axis_index("tp")}, device_id_type=MESH) for i in range(2)]
+
+
+def halves(ref):
+    rows = ref.shape[0] // 2
+    return [ref[i * rows:(i + 1) * rows] for i in range(2)]
+
+
+def send_projected(ctx, wo_ref, mine_ref, copies):
+    rows = ctx.shape[0] // 2
+    for i, copy in enumerate(copies):
+        mine_ref[i * rows:(i + 1) * rows] = dot(ctx[i * rows:(i + 1) * rows], wo_ref[...]).astype(BF16)
+        copy.start()
+
+
+def receive_sum(h_parts, mine_ref, other_ref, copies):
+    rows = mine_ref.shape[0] // 2
+    for i, copy in enumerate(copies):
+        copy.wait()
+        part = slice(i * rows, (i + 1) * rows)
+        yield add_parts(h_parts[i], mine_ref[part], other_ref[part])
 
 
 def add_parts(h_float, mine, other):
@@ -253,31 +283,36 @@
     return (h_float + delta.astype(F32)).astype(BF16).astype(F32)
 
 
-def cross_part(layer, x, mask, wq_copy, wq_ref, wo_copy, wo_ref, k_in, keys, v_in, values, q_t, acc_ref, p_ref, ctx_t):
-    heads, slots, head_dim, tokens = keys.shape
+def cross_context(x, mask, wq_copy, wq_ref, k_wait, keys, v_wait, values, q_t, acc_ref, p_ref, ctx_t, unrolled=False):
+    heads, head_dim, tokens = q_t.shape
+    slots = p_ref.shape[1]
     wq_copy.wait()
     proj = dot(x, wq_ref[...]).astype(BF16).astype(F32)
     q_t[...] = jnp.transpose(proj).reshape(heads, head_dim, tokens)
 
     def score_step(head, carry):
-        k_in(head).wait()
+        k_wait(head)
         score_head(q_t[head], keys, head, acc_ref)
         return carry
 
-    lax.fori_loop(0, heads, score_step, 0)
-    valid = mask > 0
-    for head in range(heads):
-        p_ref[head] = softmax_rows(jnp.where(valid, gather_scores(acc_ref, head, slots), NEG_BIG))
-
     def context_step(head, carry):
-        v_in(head).wait()
+        v_wait(head)
         ctx_t[head] = context_head(p_ref, values, head)
         return carry
 
-    lax.fori_loop(0, heads, context_step, 0)
-    ctx = jnp.transpose(ctx_t[...].reshape(heads * head_dim, tokens)).astype(BF16)
-    wo_copy.wait()
-    return dot(ctx, wo_ref[...]).astype(BF16)
+    def for_heads(step):
+        if unrolled:
+            for head in range(heads):
+                step(head, 0)
+        else:
+            lax.fori_loop(0, heads, step, 0)
+
+    for_heads(score_step)
+    valid = mask > 0
+    for head in range(heads):
+        p_ref[head] = softmax_rows(jnp.where(valid, gather_scores(acc_ref, head, slots), NEG_BIG))
+    for_heads(context_step)
+    return jnp.transpose(ctx_t[...].reshape(heads * head_dim, tokens)).astype(BF16)
 
 
 def middle_kernel(layer, part_ref, h_hbm, mask_hbm, scale_hbm, pos_hbm, wq_hbm, wo_hbm, k_hbm, v_hbm, dg_hbm, du_hbm, dd_hbm,
@@ -317,32 +352,37 @@
     pl.semaphore_wait(barrier, 1)
 
     copies = [tp_exchange(part_ref if i == 0 else mine_ref.at[i - 1], other_ref.at[i], send_sem.at[i], recv_sem.at[i]) for i in range(3)]
-    copies[0].start()
+    for c in copies[0]:
+        c.start()
     for c in small:
         c.wait()
-    copies[0].wait()
-    h_float = add_parts(h_ref[...].astype(F32), part_ref[...], other_ref[0])
-
-    x = rms_norm(h_float, scale_ref[1, layer:layer + 1, :])
-    mine_ref[0] = cross_part(layer, x, mask_ref[...], wq_copy, wq_ref, wo_copy, wo_ref, k_in, keys, v_in, values, q_t, acc_ref, p_ref, ctx_t)
-    copies[1].start()
-    copies[1].wait()
-    h_float = add_parts(h_float, mine_ref[0], other_ref[1])
-
-    x = rms_norm(h_float, scale_ref[2, layer:layer + 1, :])
-    dense[0].wait()
-    dense[1].wait()
+    h_parts = [h.astype(F32) for h in halves(h_ref)]
+    h_new, x_new = [], []
+    for h in receive_sum(h_parts, part_ref, other_ref.at[0], copies[0]):
+        h_new.append(h)
+        x_new.append(rms_norm(h, scale_ref[1, layer:layer + 1, :]))
+    x = jnp.concatenate(x_new, axis=0)
+    ctx = cross_context(x, mask_ref[...], wq_copy, wq_ref, lambda head: k_in(head).wait(), keys, lambda head: v_in(head).wait(), values, q_t, acc_ref, p_ref, ctx_t)
+    wo_copy.wait()
+    send_projected(ctx, wo_ref, mine_ref.at[0], copies[1])
+
+    for c in dense:
+        c.wait()
     width = dg_ref.shape[1]
     step = 512
-    for c in range(0, width, step):
-        gate_in = dot(x, dg_ref[:, c:c + step])
-        lin_in = dot(x, du_ref[:, c:c + step])
-        prod_ref[:, c:c + step] = (jax.nn.gelu(gate_in) * lin_in).astype(BF16)
-    dense[2].wait()
-    mine_ref[1] = dot(prod_ref[...], dd_ref[...]).astype(BF16)
-    copies[2].start()
-    copies[2].wait()
-    out_ref[...] = add_parts(h_float, mine_ref[1], other_ref[2]).astype(BF16)
+    rows = ctx.shape[0] // 2
+    h_last = []
+    for i, h in enumerate(receive_sum(h_new, mine_ref.at[0], other_ref.at[1], copies[1])):
+        h_last.append(h)
+        x = rms_norm(h, scale_ref[2, layer:layer + 1, :])
+        for c in range(0, width, step):
+            gate_in = dot(x, dg_ref[:, c:c + step])
+            lin_in = dot(x, du_ref[:, c:c + step])
+            prod_ref[i * rows:(i + 1) * rows, c:c + step] = (jax.nn.gelu(gate_in) * lin_in).astype(BF16)
+        mine_ref[1, i * rows:(i + 1) * rows] = dot(prod_ref[i * rows:(i + 1) * rows], dd_ref[...]).astype(BF16)
+        copies[2][i].start()
+    for i, h in enumerate(receive_sum(h_last, mine_ref.at[1], other_ref.at[2], copies[2])):
+        out_ref[i * rows:(i + 1) * rows] = h.astype(BF16)
     for c in following:
         c.wait()
 
@@ -380,7 +420,7 @@
             pltpu.VMEM((2, tokens, model), BF16),
             pltpu.VMEM((3, tokens, model), BF16),
             pltpu.VMEM((tokens, ff), BF16),
-            dma((5,)), dma((heads,)), dma((heads,)), dma((3,)), dma((3,)), dma((4,)), dma((6,)),
+            dma((5,)), dma((heads,)), dma((heads,)), dma((3, 2)), dma((3, 2)), dma((4,)), dma((6,)),
         ],
         compiler_params=pltpu.CompilerParams(vmem_limit_bytes=26 * MIB, collective_id=0, has_side_effects=True),
         name="middle",
@@ -389,10 +429,11 @@
 
 def last_kernel(layer, h_ref, part_ref, mask_hbm, idx_hbm, scale_hbm, router_hbm, wq_hbm, wo_hbm, k_hbm, v_hbm, eg_hbm, eu_hbm, ed_hbm,
                 out_ref,
-                mask_ref, idx_ref, scale_ref, router_ref, wq_ref, wo_ref, keys, values, eg_ref, eu_ref, ed_ref, q_t, acc_ref, p_ref, ctx_t, mine_ref, other_ref,
+                mask_ref, idx_ref, scale_ref, router_ref, wq_ref, wo_ref, eg_ref, eu_ref, ed_ref, q_t, acc_ref, p_ref, ctx_t, mine_ref, other_ref,
                 place_ref, send_x, recv_x, product_ref, send_y, recv_y, comb_ref, gate_ref,
                 w_sem, k_sem, v_sem, g_sem, d_sem, tp_send, tp_recv, x_send, x_recv, y_send, y_recv, s_sem):
-    heads = k_sem.shape[0]
+    heads, head_dim, _ = q_t.shape
+    slots = p_ref.shape[1]
     tokens, model = h_ref.shape
     experts = router_ref.shape[0]
     local, groups, capacity, _ = recv_x.shape
@@ -408,11 +449,37 @@
     def peer_tp(offset):
         return lax.rem(tp + offset, 2)
 
+    regions = (eg_ref.at[g_slots - 1], eu_ref.at[g_slots - 1], ed_ref.at[d_slots - 1])
+    places = []
+    for region in range(3):
+        height, wide = regions[region].shape
+        places += [(region, w, r) for w in range(wide // tokens) for r in range(height // head_dim)]
+
+    def block(number):
+        region, w, r = places[number]
+        return regions[region].at[r * head_dim:(r + 1) * head_dim, w * tokens:(w + 1) * tokens]
+
+    def cache_in(source, head, first, sems):
+        out, slot = [], 0
+        while slot < slots:
+            region, w, r = places[first + slot]
+            count = 1
+            while slot + count < slots and places[first + slot + count][:2] == (region, w):
+                count += 1
+            dst = regions[region].at[r * head_dim:(r + count) * head_dim, w * tokens:(w + 1) * tokens]
+            out.append(pltpu.make_async_copy(source.at[layer, head, slot * head_dim:(slot + count) * head_dim], dst, sems.at[head, len(out)]))
+            slot += count
+        return out
+
     def k_in(head):
-        return pltpu.make_async_copy(k_hbm.at[layer, head], keys.at[head], k_sem.at[head])
+        return cache_in(k_hbm, head, head * slots, k_sem)
 
     def v_in(head):
-        return pltpu.make_async_copy(v_hbm.at[layer, head], values.at[head], v_sem.at[head])
+        return cache_in(v_hbm, head, (heads + head) * slots, v_sem)
+
+    def wait_all(copies):
+        for c in copies:
+            c.wait()
 
     def gate_up_in(expert):
         slot = lax.rem(expert, g_slots)
@@ -435,17 +502,20 @@
         c.start()
     wq_copy.start()
     for head in range(heads):
-        k_in(head).start()
-    for head in range(heads):
-        v_in(head).start()
+        for c in k_in(head):
+            c.start()
+    for head in range(heads):
+        for c in v_in(head):
+            c.start()
     wo_copy.start()
-    for expert in range(max(g_slots, d_slots)):
-        for c in (gate_up_in(expert) if expert < g_slots else []) + ([down_in(expert)] if expert < d_slots else []):
+    for expert in range(max(g_slots, d_slots) - 1):
+        for c in (gate_up_in(expert) if expert < g_slots - 1 else []) + ([down_in(expert)] if expert < d_slots - 1 else []):
             c.start(priority=1)
     pl.semaphore_wait(barrier, len(others))
 
     copies = [tp_exchange(part_ref if i == 0 else mine_ref, other_ref.at[i], tp_send.at[i], tp_recv.at[i]) for i in range(2)]
-    copies[0].start()
+    for c in copies[0]:
+        c.start()
 
     for c in small:
         c.wait()
@@ -457,14 +527,27 @@
     row_of = jnp.where(slot_of < capacity, lax.rem(idx, local) * rows + lax.div(idx, local) * capacity + slot_of, -1)
     place_ref[...] = (lax.broadcasted_iota(jnp.int32, (experts * capacity, tokens), 0) == row_of).astype(F32).astype(BF16)
 
-    copies[0].wait()
-    h_float = add_parts(h_ref[...].astype(F32), part_ref[...], other_ref[0])
-    x = rms_norm(h_float, scale_ref[1, layer:layer + 1, :])
-    mine_ref[...] = cross_part(layer, x, mask_ref[...], wq_copy, wq_ref, wo_copy, wo_ref, k_in, keys, v_in, values, q_t, acc_ref, p_ref, ctx_t)
-    copies[1].start()
-    copies[1].wait()
-    h_float = add_parts(h_float, mine_ref[...], other_ref[1])
-    x = rms_norm(h_float, scale_ref[2, layer:layer + 1, :])
+    h_parts = [h.astype(F32) for h in halves(h_ref)]
+    h_new, x_new = [], []
+    for h in receive_sum(h_parts, part_ref, other_ref.at[0], copies[0]):
+        h_new.append(h)
+        x_new.append(rms_norm(h, scale_ref[1, layer:layer + 1, :]))
+    x = jnp.concatenate(x_new, axis=0)
+    ctx = cross_context(
+        x, mask_ref[...], wq_copy, wq_ref,
+        lambda head: wait_all(k_in(head)), lambda head, slot: block(head * slots + slot)[...],
+        lambda head: wait_all(v_in(head)), lambda head, slot: block((heads + head) * slots + slot)[...],
+        q_t, acc_ref, p_ref, ctx_t, True)
+    for c in gate_up_in(g_slots - 1) + [down_in(d_slots - 1)]:
+        c.start(priority=1)
+    wo_copy.wait()
+    send_projected(ctx, wo_ref, mine_ref, copies[1])
+    h_last, x_new = [], []
+    for h in receive_sum(h_new, mine_ref, other_ref.at[1], copies[1]):
+        h_last.append(h)
+        x_new.append(rms_norm(h, scale_ref[2, layer:layer + 1, :]))
+    h_float = jnp.concatenate(h_last, axis=0)
+    x = jnp.concatenate(x_new, axis=0)
 
     def x_copy(expert, offset):
         return pltpu.make_async_remote_copy(
@@ -577,6 +660,7 @@
 
 def last(layer, h, part, mask, idx, scale, router, w_query, w_out, keys, values, exp_gate, exp_up, exp_down, groups):
     _, heads, slots, head_dim, tokens = keys.shape
+    flat = keys.shape[:2] + (slots * head_dim, tokens)
     width, model = w_out.shape[1:]
     local, _, ff = exp_gate.shape
     experts = router.shape[0]
@@ -597,8 +681,6 @@
             pltpu.VMEM(router.shape, F32),
             pltpu.VMEM((model, width), BF16),
             pltpu.VMEM((width, model), BF16),
-            pltpu.VMEM((heads, slots, head_dim, tokens), BF16),
-            pltpu.VMEM((heads, slots, head_dim, tokens), BF16),
             pltpu.VMEM((GATE_SLOTS, model, ff), BF16),
             pltpu.VMEM((GATE_SLOTS, model, ff), BF16),
             pltpu.VMEM((DOWN_SLOTS, ff, model), BF16),
@@ -616,12 +698,12 @@
             pltpu.VMEM((local, 2 * groups, capacity, model), BF16),
             pltpu.VMEM((experts * capacity, model), BF16),
             pltpu.VMEM((tokens, tokens), F32),
-            dma((2,)), dma((heads,)), dma((heads,)), dma((GATE_SLOTS, 2)), dma((DOWN_SLOTS,)), dma((2,)), dma((2,)),
+            dma((2,)), dma((heads, 4)), dma((heads, 4)), dma((GATE_SLOTS, 2)), dma((DOWN_SLOTS,)), dma((2, 2)), dma((2, 2)),
             dma((local,)), dma((local,)), dma((local,)), dma((local,)), dma((4,)),
         ],
         compiler_params=pltpu.CompilerParams(vmem_limit_bytes=LAST_VMEM, collective_id=1, has_side_effects=True),
         name="last",
-    )(on_chip(h), on_chip(part), *map(pinned, (mask, idx, scale, router, w_query, w_out, keys, values, exp_gate, exp_up, exp_down)))
+    )(on_chip(h), on_chip(part), *map(pinned, (mask, idx, scale, router, w_query, w_out, keys.reshape(flat), values.reshape(flat), exp_gate, exp_up, exp_down)))
 
 
 def decode_body(groups, hidden, write_pos, enc_mask, expert_idx, self_keys, self_values, cross_keys, cross_values, rel_bias, norm_scale, w_query, w_key, w_value, w_out, w_cross_query, w_cross_out, dense_gate, dense_up, dense_down, router, exp_gate, exp_up, exp_down):
@@ -633,10 +715,10 @@
     mask = jnp.transpose(enc_mask)
     scale = jnp.transpose(norm_scale, (1, 0, 2))
     keys, values, ckeys, cvalues = map(lanes, (self_keys, self_values, cross_keys, cross_values))
-    part, bias, k_out, v_out = self_first(0, hidden, pos, scale, rel_bias, w_query, w_key, w_value, w_out, keys, values)
+    part, bias, k_out, v_first = self_first(0, hidden, pos, scale, rel_bias, w_query, w_key, w_value, w_out, keys, values)
     following = (w_query, w_key, w_value, w_out, keys, values)
     h, pos, scale_in, w_in, w_o, keys, values = middle(0, part, hidden, mask, scale, pos, w_cross_query, w_cross_out, ckeys, cvalues, dense_gate, dense_up, dense_down, following)
-    part, k_out, v_out = self_second(1, h, pos, scale_in, bias, w_in, w_o, keys, values, k_out, v_out)
+    part, k_out, v_out = self_second(1, h, pos, scale_in, bias, w_in, w_o, keys, values, v_first, k_out)
     h = last(1, h, part, mask, idx, scale, jnp.transpose(router), w_cross_query, w_cross_out, ckeys, cvalues, exp_gate, exp_up, exp_down, groups)
     return h, jnp.transpose(k_out, (0, 4, 1, 2, 3)), jnp.transpose(v_out, (0, 4, 1, 2, 3))
 

time: 79.2 us -> 76 us (0.960)
  Pallas kernels: 77.7 us -> 74.6 us
    pallas_call x1, Pallas kernels: 44.5 us -> 42.6 us  [last(): pl.pallas_call(functools.partial(last_kernel, layer), out_shape=pltpu.VME...]
    pallas_call x1, Pallas kernels: 22.9 us -> 22.1 us  [middle(): pl.pallas_call(functools.partial(middle_kernel, layer), out_shape=[pltpu....]
where the time goes in v4:
time: 76 us; the launch traced here: 75.9 us
  Pallas kernels  74.6 us (98%)
    pallas_call x1, Pallas kernels, last(): pl.pallas_call(functools.partial(last_kernel, layer), out_shape=pltpu.VME...  42.6 us
    pallas_call x1, Pallas kernels, middle(): pl.pallas_call(functools.partial(middle_kernel, layer), out_shape=[pltpu....  22.1 us
    pallas_call x1, Pallas kernels, self_first(): pl.pallas_call(functools.partial(first_kernel, layer), out_shape=[pltpu.V...  6.03 us
    pallas_call x1, Pallas kernels, self_second(): pl.pallas_call(functools.partial(second_kernel, layer), out_shape=[pltpu....  3.86 us

profile of v4, /device:TPU:0, one launch (start us, length us, event | category | flops | bytes accessed | tf_op | source)
XLA Modules:
  0.0 75.9 jit_solution(7851775550874992084)
XLA Ops:
  0.6 6.0 %self_first.1 = (bf16[128,768]{1,0:T(8,128)(2,1)S(1)}, f32[6,32,128]{2,1,0:T(8,128)S(1)}, bf16[2,6,32,64,128]{4,3,2,1,0:T(8,128)(2,1)}, bf16[6,32,64,128]{3,2,1,0:T(8,128)(2,1)S(1)}) custom-call(bf16[128,768]{1,0:T(8,128)(2,1)} %h_hbm.3, s32[1,128]{1,0:T(1,128)} %bitcast.30, f32[3,2,768]{2,1,0:T(2,128)} %bitcast.25, f32[6,32]{1,0:T(8,128)} %rel_hbm.1, ...), custom_call_target="tpu_custom_call" | custom-call | tf_op jit(solution)/shard_map/self_first/pallas_call | solution.py:212
  6.7 22.1 %middle.1 = (bf16[128,768]{1,0:T(8,128)(2,1)S(1)}, s32[1,128]{1,0:T(1,128)S(1)}, f32[3,2,768]{2,1,0:T(2,128)S(1)}, bf16[3,768,384]{2,1,0:T(8,128)(2,1)S(1)}, bf1...) custom-call(bf16[128,768]{1,0:T(8,128)(2,1)S(1)} %get-tuple-element.17.part_ref, ...), custom_call_target="tpu_custom_call" | custom-call | tf_op jit(solution)/shard_map/middle/pallas_call | solution.py:398
  28.8 3.9 %self_second.1 = (bf16[128,768]{1,0:T(8,128)(2,1)S(1)}, bf16[2,6,32,64,128]{4,3,2,1,0:T(8,128)(2,1)}, bf16[2,6,32,64,128]{4,3,2,1,0:T(8,128)(2,1)}) custom-call(bf16[128,768]{1,0:T(8,128)(2,1)S(1)} %get-tuple-element.18.h_ref, s32[1,128]{1,0:T(1,128)S(1)} %get-tuple-element.19.pos_ref, ...), custom_call_target="tpu_custom_call", output_to_operand_aliasing={{1}: (9, {})} | custom-call | tf_op jit(solution)/shard_map/self_second/pallas_call | solution.py:241
  32.6 42.6 %last.1 = bf16[128,768]{1,0:T(8,128)(2,1)S(1)} custom-call(bf16[128,768]{1,0:T(8,128)(2,1)S(1)} %get-tuple-element.18.h_ref, bf16[128,768]{1,0:T(8,128)(2,1)S(1)} %get-tuple-element.28.part_ref, s32[32,128]{1,0:T(8,128)} %bitcast.29, s32[1,128]{1,0:T(1,128)} %bitcast.32, f32[3,2,768]{2,1,0:T(2,128)} %bitcast.27, f32[64,768]{1,0:T(8,128)} %bitcast.24, ...), custom_call_target="tpu_custom_call" | custom-call | tf_op jit(solution)/shard_map/last/pallas_call | solution.py:672
  75.3 0.7 copy.29

commit v5 on v4

--- a/solution.py
+++ b/solution.py
@@ -13,9 +13,10 @@
 BF16 = jnp.bfloat16
 F32 = jnp.float32
 MIB = 1024 * 1024
-GATE_SLOTS = 8
-DOWN_SLOTS = 8
-LAST_VMEM = 62 * MIB
+GATE_SLOTS = 7
+DOWN_SLOTS = 7
+KEPT = 1
+LAST_VMEM = int(53.5 * MIB)
 
 
 def rms_norm(h_float, scale):
@@ -82,57 +83,18 @@
     return pltpu.with_memory_space_constraint(x, pltpu.HBM)
 
 
-def first_kernel(layer, h_hbm, pos_hbm, scale_hbm, rel_hbm, wq_hbm, wk_hbm, wv_hbm, wo_hbm, k_hbm, v_hbm,
-                 part_ref, bias_ref, ko_hbm, values,
-                 h_ref, pos_ref, scale_ref, rel_ref, w_in, wo_ref, keys, q_t, k_t, v_t, acc_ref, p_ref, ctx_t,
-                 s_sem, w_sem, k_sem, v_sem, ko_sem):
-    heads = keys.shape[0]
-    small = [pltpu.make_async_copy(s, d, s_sem.at[i]) for i, (s, d) in enumerate(
-        ((h_hbm, h_ref), (scale_hbm, scale_ref), (pos_hbm, pos_ref), (rel_hbm, rel_ref)))]
-    w_copies = [pltpu.make_async_copy(w.at[layer], w_in.at[i], w_sem.at[i]) for i, w in enumerate((wq_hbm, wk_hbm, wv_hbm))]
-    wo_copy = pltpu.make_async_copy(wo_hbm.at[layer], wo_ref, w_sem.at[3])
-
-    def k_in(head):
-        return pltpu.make_async_copy(k_hbm.at[layer, head], keys.at[head], k_sem.at[head])
-
-    def v_in(head):
-        return pltpu.make_async_copy(v_hbm.at[layer, head], values.at[head], v_sem.at[head])
-
-    for c in small + w_copies:
-        c.start()
-    for head in range(heads):
-        k_in(head).start()
-    for head in range(heads):
-        v_in(head).start(priority=1)
-    wo_copy.start(priority=1)
-
-    slots, tokens = bias_ref.shape[1:]
-    small[2].wait()
-    small[3].wait()
-    dist = pos_ref[...] - lax.broadcasted_iota(jnp.int32, (slots, tokens), 0)
-    bias = [jnp.zeros((slots, tokens), F32)] * heads
-    for d in range(slots):
-        hit = dist == d
-        bias = [jnp.where(hit, rel_ref[head, d], b) for head, b in enumerate(bias)]
-    for head in range(heads):
-        bias_ref[head] = bias[head]
-    small[0].wait()
-    small[1].wait()
-
-    self_part(layer, h_ref, pos_ref, scale_ref, bias_ref, w_in, [c.wait for c in w_copies], wo_ref, wo_copy.wait,
-              keys, values, lambda head: k_in(head).wait(), lambda head: v_in(head).wait(), keys, values,
-              part_ref, ko_hbm, None, q_t, k_t, v_t, acc_ref, p_ref, ctx_t, ko_sem, None)
-
-
-def second_kernel(layer, h_ref, pos_ref, scale_ref, bias_ref, w_in, wo_ref, keys_in, values_in, values_before, _,
+def second_kernel(layer, h_ref, pos_ref, scale_ref, bias_ref, w_in, wo_ref, keys_in, values_in, keys_before, values_before,
                   part_ref, ko_hbm, vo_hbm,
                   keys, values, q_t, k_t, v_t, acc_ref, p_ref, ctx_t, ko_sem, vo_sem, before_sem):
-    before = pltpu.make_async_copy(values_before, vo_hbm.at[layer - 1], before_sem)
-    before.start()
+    before = [pltpu.make_async_copy(s, d.at[layer - 1], before_sem.at[i])
+              for i, (s, d) in enumerate(((keys_before, ko_hbm), (values_before, vo_hbm)))]
+    for c in before:
+        c.start()
     self_part(layer, h_ref, pos_ref, scale_ref, bias_ref, w_in, [None] * 3, wo_ref, None,
               keys_in, values_in, None, None, keys, values,
               part_ref, ko_hbm, vo_hbm, q_t, k_t, v_t, acc_ref, p_ref, ctx_t, ko_sem, vo_sem)
-    before.wait()
+    for c in before:
+        c.wait()
 
 
 def self_part(layer, h_ref, pos_ref, scale_ref, bias_ref, w_in, w_waits, wo_ref, wo_wait,
@@ -161,7 +123,8 @@
         if k_wait is not None:
             k_wait(head)
         score_head(q_t[head], keys_in, head, acc_ref, (pos_b, k_t[head], keys))
-        k_out(head).start()
+        if ko_hbm is not None:
+            k_out(head).start()
         return carry
 
     lax.fori_loop(0, heads, score_step, 0)
@@ -182,9 +145,9 @@
     if wo_wait is not None:
         wo_wait()
     part_ref[...] = dot(ctx, wo_ref[...]).astype(BF16)
-    for head in range(heads):
-        k_out(head).wait()
-        if vo_hbm is not None:
+    if ko_hbm is not None:
+        for head in range(heads):
+            k_out(head).wait()
             v_out(head).wait()
 
 
@@ -201,53 +164,21 @@
     ]
 
 
-def self_first(layer, h, pos, scale, rel, w_query, w_key, w_value, w_out, keys, values):
-    _, heads, slots, head_dim, tokens = keys.shape
-    width, model = w_out.shape[1:]
-    vmem = pl.BlockSpec(memory_space=pltpu.VMEM)
-    hbm = pl.BlockSpec(memory_space=pltpu.HBM)
-    dma = pltpu.SemaphoreType.DMA
-    ins = [pinned(x) for x in (h, pos, scale, rel, w_query, w_key, w_value, w_out, keys, values)]
-    cache = pltpu.HBM(keys.shape, keys.dtype)
-    return pl.pallas_call(
-        functools.partial(first_kernel, layer),
-        out_shape=[
-            pltpu.VMEM((tokens, model), BF16), pltpu.VMEM((heads, slots, tokens), F32), cache,
-            pltpu.VMEM((heads, slots, head_dim, tokens), BF16),
-        ],
-        in_specs=[hbm] * 10,
-        out_specs=[vmem, vmem, hbm, vmem],
-        scratch_shapes=[
-            pltpu.VMEM((tokens, model), BF16),
-            pltpu.VMEM(pos.shape, pos.dtype),
-            pltpu.VMEM(scale.shape, F32),
-            pltpu.SMEM(rel.shape, F32),
-            pltpu.VMEM((3, model, width), BF16),
-            pltpu.VMEM((width, model), BF16),
-        ] + attention_scratch(heads, slots, head_dim, tokens)[1:] + [
-            dma((4,)), dma((4,)), dma((heads,)), dma((heads,)), dma((heads,)),
-        ],
-        compiler_params=pltpu.CompilerParams(vmem_limit_bytes=20 * MIB),
-        name="self_first",
-    )(*ins)
-
-
-def self_second(layer, h, pos, scale, bias, w_in, w_out, keys_in, values_in, values_before, k_out):
+def self_second(layer, h, pos, scale, bias, w_in, w_out, keys_in, values_in, keys_before, values_before):
     heads, slots, head_dim, tokens = keys_in.shape
     vmem = pl.BlockSpec(memory_space=pltpu.VMEM)
     hbm = pl.BlockSpec(memory_space=pltpu.HBM)
     dma = pltpu.SemaphoreType.DMA
-    cache = pltpu.HBM(k_out.shape, k_out.dtype)
+    cache = pltpu.HBM((layer + 1,) + keys_in.shape, BF16)
     return pl.pallas_call(
         functools.partial(second_kernel, layer),
         out_shape=[pltpu.VMEM(h.shape, BF16), cache, cache],
-        in_specs=[vmem] * 9 + [hbm],
+        in_specs=[vmem] * 10,
         out_specs=[vmem, hbm, hbm],
-        input_output_aliases={9: 1},
-        scratch_shapes=attention_scratch(heads, slots, head_dim, tokens) + [dma((heads,)), dma((heads,)), dma],
-        compiler_params=pltpu.CompilerParams(vmem_limit_bytes=20 * MIB),
+        scratch_shapes=attention_scratch(heads, slots, head_dim, tokens) + [dma((heads,)), dma((heads,)), dma((2,))],
+        compiler_params=pltpu.CompilerParams(vmem_limit_bytes=11 * MIB),
         name="self_second",
-    )(h, pos, scale, bias, w_in, w_out, keys_in, values_in, values_before, pinned(k_out))
+    )(h, pos, scale, bias, w_in, w_out, keys_in, values_in, keys_before, values_before)
 
 
 def tp_exchange(src, dst, send_sem, recv_sem):
@@ -283,7 +214,7 @@
     return (h_float + delta.astype(F32)).astype(BF16).astype(F32)
 
 
-def cross_context(x, mask, wq_copy, wq_ref, k_wait, keys, v_wait, values, q_t, acc_ref, p_ref, ctx_t, unrolled=False):
+def cross_context(x, mask, wq_copy, wq_ref, k_wait, keys, v_wait, values, q_t, acc_ref, p_ref, send_head, unrolled=False):
     heads, head_dim, tokens = q_t.shape
     slots = p_ref.shape[1]
     wq_copy.wait()
@@ -297,7 +228,7 @@
 
     def context_step(head, carry):
         v_wait(head)
-        ctx_t[head] = context_head(p_ref, values, head)
+        send_head(head, context_head(p_ref, values, head))
         return carry
 
     def for_heads(step):
@@ -312,20 +243,72 @@
     for head in range(heads):
         p_ref[head] = softmax_rows(jnp.where(valid, gather_scores(acc_ref, head, slots), NEG_BIG))
     for_heads(context_step)
-    return jnp.transpose(ctx_t[...].reshape(heads * head_dim, tokens)).astype(BF16)
-
-
-def middle_kernel(layer, part_ref, h_hbm, mask_hbm, scale_hbm, pos_hbm, wq_hbm, wo_hbm, k_hbm, v_hbm, dg_hbm, du_hbm, dd_hbm,
-                  nq_hbm, nk_hbm, nv_hbm, no_hbm, nkeys_hbm, nvalues_hbm,
-                  out_ref, pos_ref, scale_ref, nw_ref, nwo_ref, nkeys_ref, nvalues_ref,
-                  h_ref, mask_ref, wq_ref, wo_ref, keys, values, dg_ref, du_ref, dd_ref, q_t, acc_ref, p_ref, ctx_t, mine_ref, other_ref, prod_ref,
-                  w_sem, k_sem, v_sem, send_sem, recv_sem, s_sem, n_sem):
-    heads = keys.shape[0]
+
+
+def head_copy(ctx_ref, head, send_sem, recv_sem):
+    tp = lax.axis_index("tp")
+    return pltpu.make_async_remote_copy(
+        src_ref=ctx_ref.at[tp, head], dst_ref=ctx_ref.at[tp, head], send_sem=send_sem.at[head], recv_sem=recv_sem.at[head],
+        device_id={"tp": 1 - tp}, device_id_type=MESH)
+
+
+def project_half(ctx_ref, full_ref, half):
+    _, heads, head_dim, tokens = ctx_ref.shape
+    ctx = jnp.transpose(ctx_ref[half].astype(F32).reshape(heads * head_dim, tokens)).astype(BF16)
+    return dot(ctx, full_ref[half].reshape(heads * head_dim, full_ref.shape[-1]))
+
+
+def add_heads(h_float, mine, ctx_ref, full_ref, send_sem, recv_sem):
+    for head in range(ctx_ref.shape[1]):
+        head_copy(ctx_ref, head, send_sem, recv_sem).wait()
+    delta = (mine + project_half(ctx_ref, full_ref, 1 - lax.axis_index("tp"))).astype(BF16)
+    return (h_float + delta.astype(F32)).astype(BF16).astype(F32)
+
+
+def weight_copy(full_ref, sems):
+    tp, ep = lax.axis_index("tp"), lax.axis_index("ep")
+    return pltpu.make_async_remote_copy(
+        src_ref=full_ref.at[tp, ep], dst_ref=full_ref.at[tp, ep], send_sem=sems.at[0], recv_sem=sems.at[1],
+        device_id={"tp": 1 - tp}, device_id_type=MESH)
+
+
+def weight_forward(full_ref, offset, sems):
+    tp, ep = lax.axis_index("tp"), lax.axis_index("ep")
+    return pltpu.make_async_remote_copy(
+        src_ref=full_ref.at[1 - tp, ep], dst_ref=full_ref.at[1 - tp, ep], send_sem=sems.at[2 * offset], recv_sem=sems.at[2 * offset + 1],
+        device_id={"ep": lax.rem(ep + offset, full_ref.shape[1])}, device_id_type=MESH)
+
+
+def fill_bias(dist, rel_ref, bias_ref):
+    heads, slots, tokens = bias_ref.shape
+    bias = [jnp.zeros((slots, tokens), F32)] * heads
+    for d in range(slots):
+        hit = dist == d
+        bias = [jnp.where(hit, rel_ref[head, d], b) for head, b in enumerate(bias)]
+    for head in range(heads):
+        bias_ref[head] = bias[head]
+
+
+def middle_kernel(layer, h_hbm, mask_hbm, scale_hbm, pos_hbm, rel_hbm, sq_hbm, sk_hbm, sv_hbm, so_hbm, skeys_hbm, svalues_hbm,
+                  wq_hbm, wo_hbm, wf_hbm, k_hbm, v_hbm, dg_hbm, du_hbm, dd_hbm, eg_hbm, eu_hbm, ed_hbm,
+                  out_ref, pos_ref, scale_ref, bias_ref, nw_ref, nwo_ref, nkeys_ref, nvalues_ref, skeys, svalues, next_full, lg_ref, lu_ref, ld_ref,
+                  h_ref, mask_ref, rel_ref, sw_ref, so_ref, wq_ref, wo_ref, keys, values, dg_ref, du_ref, dd_ref,
+                  q_t, k_t, v_t, acc_ref, p_ref, ctx_t, part_ref, mine_ref, other_ref, prod_ref,
+                  w_sem, k_sem, v_sem, send_sem, recv_sem, s_sem, n_sem, sw_sem, sk_sem, sv_sem, next_sem, l_sem):
+    heads, slots, tokens = bias_ref.shape
     small = [pltpu.make_async_copy(s, d, s_sem.at[i]) for i, (s, d) in enumerate(
-        ((h_hbm, h_ref), (mask_hbm, mask_ref), (scale_hbm, scale_ref), (pos_hbm, pos_ref)))]
-    following = [pltpu.make_async_copy(s, d, n_sem.at[i]) for i, (s, d) in enumerate(
-        ((nq_hbm.at[layer + 1], nw_ref.at[0]), (nk_hbm.at[layer + 1], nw_ref.at[1]), (nv_hbm.at[layer + 1], nw_ref.at[2]),
-         (no_hbm.at[layer + 1], nwo_ref), (nkeys_hbm.at[layer + 1], nkeys_ref), (nvalues_hbm.at[layer + 1], nvalues_ref)))]
+        ((h_hbm, h_ref), (scale_hbm, scale_ref), (pos_hbm, pos_ref), (rel_hbm, rel_ref), (mask_hbm, mask_ref)))]
+    following = [pltpu.make_async_copy(s.at[layer + 1], d, n_sem.at[i]) for i, (s, d) in enumerate(
+        ((sq_hbm, nw_ref.at[0]), (sk_hbm, nw_ref.at[1]), (sv_hbm, nw_ref.at[2]),
+         (so_hbm, nwo_ref), (skeys_hbm, nkeys_ref), (svalues_hbm, nvalues_ref)))]
+    own = [pltpu.make_async_copy(s.at[layer], d, sw_sem.at[i]) for i, (s, d) in enumerate(
+        ((sq_hbm, sw_ref.at[0]), (sk_hbm, sw_ref.at[1]), (sv_hbm, sw_ref.at[2]), (so_hbm, so_ref)))]
+
+    def sk_in(head):
+        return pltpu.make_async_copy(skeys_hbm.at[layer, head], skeys.at[head], sk_sem.at[head])
+
+    def sv_in(head):
+        return pltpu.make_async_copy(svalues_hbm.at[layer, head], svalues.at[head], sv_sem.at[head])
 
     def k_in(head):
         return pltpu.make_async_copy(k_hbm.at[layer, head], keys.at[head], k_sem.at[head])
@@ -334,35 +317,68 @@
         return pltpu.make_async_copy(v_hbm.at[layer, head], values.at[head], v_sem.at[head])
 
     wq_copy = pltpu.make_async_copy(wq_hbm.at[layer], wq_ref, w_sem.at[0])
+    tp, ep = lax.axis_index("tp"), lax.axis_index("ep")
+    groups = next_full.shape[1]
     wo_copy = pltpu.make_async_copy(wo_hbm.at[layer], wo_ref, w_sem.at[1])
+    next_copy = pltpu.make_async_copy(wf_hbm.at[layer + 1], next_full.at[tp], w_sem.at[5])
     dense = [pltpu.make_async_copy(s, d, w_sem.at[2 + i]) for i, (s, d) in enumerate(((dg_hbm, dg_ref), (du_hbm, du_ref), (dd_hbm, dd_ref)))]
 
+    kept = lg_ref.shape[0]
+    first_kept = eg_hbm.shape[0] - kept
+    late = [pltpu.make_async_copy(s.at[first_kept + i], d.at[i], l_sem.at[i, j])
+            for i in range(kept) for j, (s, d) in enumerate(((eg_hbm, lg_ref), (eu_hbm, lu_ref), (ed_hbm, ld_ref)))]
+
+    for c in small + own[:3]:
+        c.start()
     barrier = pltpu.get_barrier_semaphore()
-    pl.semaphore_signal(barrier, inc=1, device_id={"tp": 1 - lax.axis_index("tp")}, device_id_type=MESH)
-    for c in small:
-        c.start()
-    wq_copy.start()
-    for head in range(heads):
-        k_in(head).start()
+    pl.semaphore_signal(barrier, inc=1, device_id={"tp": 1 - tp}, device_id_type=MESH)
+    for offset in range(1, groups):
+        pl.semaphore_signal(barrier, inc=1, device_id={"ep": lax.rem(ep + offset, groups)}, device_id_type=MESH)
+    next_copy.start()
+    for head in range(heads):
+        sk_in(head).start()
+    for head in range(heads):
+        sv_in(head).start()
+    own[3].start()
+    wq_copy.start(priority=1)
+    for head in range(heads):
+        k_in(head).start(priority=1)
     for head in range(heads):
         v_in(head).start(priority=1)
     wo_copy.start(priority=1)
-    for c in dense + following:
+    for c in dense + following + late:
         c.start(priority=1)
-    pl.semaphore_wait(barrier, 1)
+
+    small[2].wait()
+    small[3].wait()
+    fill_bias(pos_ref[...] - lax.broadcasted_iota(jnp.int32, (slots, tokens), 0), rel_ref, bias_ref)
+    for i in (0, 1, 4):
+        small[i].wait()
+    next_copy.wait()
+    pl.semaphore_wait(barrier, groups)
+    weight_copy(next_full, next_sem).start()
+    self_part(layer, h_ref, pos_ref, scale_ref, bias_ref, sw_ref, [c.wait for c in own[:3]], so_ref, own[3].wait,
+              skeys, svalues, lambda head: sk_in(head).wait(), lambda head: sv_in(head).wait(), skeys, svalues,
+              part_ref, None, None, q_t, k_t, v_t, acc_ref, p_ref, ctx_t, None, None)
 
     copies = [tp_exchange(part_ref if i == 0 else mine_ref.at[i - 1], other_ref.at[i], send_sem.at[i], recv_sem.at[i]) for i in range(3)]
     for c in copies[0]:
         c.start()
-    for c in small:
-        c.wait()
+    weight_copy(next_full, next_sem).wait_recv()
+    for offset in range(1, groups):
+        weight_forward(next_full, offset, next_sem).start()
     h_parts = [h.astype(F32) for h in halves(h_ref)]
     h_new, x_new = [], []
     for h in receive_sum(h_parts, part_ref, other_ref.at[0], copies[0]):
         h_new.append(h)
         x_new.append(rms_norm(h, scale_ref[1, layer:layer + 1, :]))
     x = jnp.concatenate(x_new, axis=0)
-    ctx = cross_context(x, mask_ref[...], wq_copy, wq_ref, lambda head: k_in(head).wait(), keys, lambda head: v_in(head).wait(), values, q_t, acc_ref, p_ref, ctx_t)
+
+    def keep_head(head, ctx):
+        ctx_t[head] = ctx
+
+    cross_context(x, mask_ref[...], wq_copy, wq_ref, lambda head: k_in(head).wait(), keys, lambda head: v_in(head).wait(), values, q_t, acc_ref, p_ref, keep_head)
+    ctx = jnp.transpose(ctx_t[...].reshape(wo_ref.shape[0], tokens)).astype(BF16)
     wo_copy.wait()
     send_projected(ctx, wo_ref, mine_ref.at[0], copies[1])
 
@@ -383,29 +399,39 @@
         copies[2][i].start()
     for i, h in enumerate(receive_sum(h_last, mine_ref.at[1], other_ref.at[2], copies[2])):
         out_ref[i * rows:(i + 1) * rows] = h.astype(BF16)
-    for c in following:
+    for c in following + late:
         c.wait()
-
-
-def middle(layer, part, h, mask, scale, pos, w_query, w_out, keys, values, dense_gate, dense_up, dense_down, following):
+    weight_copy(next_full, next_sem).wait_send()
+    for offset in range(1, groups):
+        weight_forward(next_full, offset, next_sem).wait()
+
+
+def middle(layer, h, mask, scale, pos, rel, w_self, keys_self, values_self, w_query, w_out, w_full, keys, values, dense_gate, dense_up, dense_down, experts):
     _, heads, slots, head_dim, tokens = keys.shape
-    width, model = w_out.shape[1:]
+    width, model = w_self[3].shape[1:]
+    full = (2,) + w_full.shape[1:]
     ff = dense_gate.shape[1]
     vmem = pl.BlockSpec(memory_space=pltpu.VMEM)
     hbm = pl.BlockSpec(memory_space=pltpu.HBM)
     dma = pltpu.SemaphoreType.DMA
     cache = pltpu.VMEM((heads, slots, head_dim, tokens), BF16)
+    ins = (h, mask, scale, pos, rel) + w_self + (keys_self, values_self, w_query, w_out, w_full, keys, values, dense_gate, dense_up, dense_down) + experts
+    outs = [
+        pltpu.VMEM((tokens, model), BF16), pltpu.VMEM(pos.shape, pos.dtype), pltpu.VMEM(scale.shape, F32), pltpu.VMEM((heads, slots, tokens), F32),
+        pltpu.VMEM((3, model, width), BF16), pltpu.VMEM((width, model), BF16), cache, cache, cache, cache, pltpu.VMEM(full, BF16),
+        pltpu.VMEM((KEPT, model, ff), BF16), pltpu.VMEM((KEPT, model, ff), BF16), pltpu.VMEM((KEPT, ff, model), BF16),
+    ]
     return pl.pallas_call(
         functools.partial(middle_kernel, layer),
-        out_shape=[
-            pltpu.VMEM((tokens, model), BF16), pltpu.VMEM(pos.shape, pos.dtype), pltpu.VMEM(scale.shape, F32),
-            pltpu.VMEM((3, model, width), BF16), pltpu.VMEM((width, model), BF16), cache, cache,
-        ],
-        in_specs=[vmem] + [hbm] * 17,
-        out_specs=[vmem] * 7,
+        out_shape=outs,
+        in_specs=[hbm] * len(ins),
+        out_specs=[vmem] * len(outs),
         scratch_shapes=[
             pltpu.VMEM((tokens, model), BF16),
             pltpu.VMEM(mask.shape, mask.dtype),
+            pltpu.SMEM(rel.shape, F32),
+            pltpu.VMEM((3, model, width), BF16),
+            pltpu.VMEM((width, model), BF16),
             pltpu.VMEM((model, width), BF16),
             pltpu.VMEM((width, model), BF16),
             pltpu.VMEM((heads, slots, head_dim, tokens), BF16),
@@ -413,25 +439,23 @@
             pltpu.VMEM((model, ff), BF16),
             pltpu.VMEM((model, ff), BF16),
             pltpu.VMEM((ff, model), BF16),
-            pltpu.VMEM((heads, head_dim, tokens), F32),
-            pltpu.VMEM((heads, slots * 8, tokens), F32),
-            pltpu.VMEM((heads, slots, tokens), F32),
-            pltpu.VMEM((heads, head_dim, tokens), F32),
+        ] + attention_scratch(heads, slots, head_dim, tokens)[2:] + [
+            pltpu.VMEM((tokens, model), BF16),
             pltpu.VMEM((2, tokens, model), BF16),
             pltpu.VMEM((3, tokens, model), BF16),
             pltpu.VMEM((tokens, ff), BF16),
-            dma((5,)), dma((heads,)), dma((heads,)), dma((3, 2)), dma((3, 2)), dma((4,)), dma((6,)),
+            dma((6,)), dma((heads,)), dma((heads,)), dma((3, 2)), dma((3, 2)), dma((5,)), dma((6,)), dma((4,)), dma((heads,)), dma((heads,)), dma((2 * full[1],)), dma((KEPT, 3)),
         ],
-        compiler_params=pltpu.CompilerParams(vmem_limit_bytes=26 * MIB, collective_id=0, has_side_effects=True),
+        compiler_params=pltpu.CompilerParams(vmem_limit_bytes=22 * MIB, collective_id=0, has_side_effects=True),
         name="middle",
-    )(part, *map(pinned, (h, mask, scale, pos, w_query, w_out, keys, values, dense_gate, dense_up, dense_down) + following))
-
-
-def last_kernel(layer, h_ref, part_ref, mask_hbm, idx_hbm, scale_hbm, router_hbm, wq_hbm, wo_hbm, k_hbm, v_hbm, eg_hbm, eu_hbm, ed_hbm,
+    )(*map(pinned, ins))
+
+
+def last_kernel(layer, h_ref, part_ref, full_ref, lg_ref, lu_ref, ld_ref, mask_hbm, idx_hbm, scale_hbm, router_hbm, wq_hbm, k_hbm, v_hbm, eg_hbm, eu_hbm, ed_hbm,
                 out_ref,
-                mask_ref, idx_ref, scale_ref, router_ref, wq_ref, wo_ref, eg_ref, eu_ref, ed_ref, q_t, acc_ref, p_ref, ctx_t, mine_ref, other_ref,
+                mask_ref, idx_ref, scale_ref, router_ref, wq_ref, eg_ref, eu_ref, ed_ref, q_t, acc_ref, p_ref, ctx_ref, other_ref,
                 place_ref, send_x, recv_x, product_ref, send_y, recv_y, comb_ref, gate_ref,
-                w_sem, k_sem, v_sem, g_sem, d_sem, tp_send, tp_recv, x_send, x_recv, y_send, y_recv, s_sem):
+                w_sem, k_sem, v_sem, g_sem, d_sem, tp_send, tp_recv, x_send, x_recv, y_send, y_recv, s_sem, c_send, c_recv):
     heads, head_dim, _ = q_t.shape
     slots = p_ref.shape[1]
     tokens, model = h_ref.shape
@@ -492,7 +516,6 @@
     small = [pltpu.make_async_copy(s, d, s_sem.at[i]) for i, (s, d) in enumerate(
         ((mask_hbm, mask_ref), (idx_hbm, idx_ref), (scale_hbm, scale_ref), (router_hbm, router_ref)))]
     wq_copy = pltpu.make_async_copy(wq_hbm.at[layer], wq_ref, w_sem.at[0])
-    wo_copy = pltpu.make_async_copy(wo_hbm.at[layer], wo_ref, w_sem.at[1])
 
     others = [(dt, de) for dt in range(2) for de in range(groups) if dt or de]
     barrier = pltpu.get_barrier_semaphore()
@@ -507,14 +530,13 @@
     for head in range(heads):
         for c in v_in(head):
             c.start()
-    wo_copy.start()
     for expert in range(max(g_slots, d_slots) - 1):
         for c in (gate_up_in(expert) if expert < g_slots - 1 else []) + ([down_in(expert)] if expert < d_slots - 1 else []):
             c.start(priority=1)
     pl.semaphore_wait(barrier, len(others))
 
-    copies = [tp_exchange(part_ref if i == 0 else mine_ref, other_ref.at[i], tp_send.at[i], tp_recv.at[i]) for i in range(2)]
-    for c in copies[0]:
+    copies = tp_exchange(part_ref, other_ref, tp_send, tp_recv)
+    for c in copies:
         c.start()
 
     for c in small:
@@ -529,25 +551,25 @@
 
     h_parts = [h.astype(F32) for h in halves(h_ref)]
     h_new, x_new = [], []
-    for h in receive_sum(h_parts, part_ref, other_ref.at[0], copies[0]):
+    for h in receive_sum(h_parts, part_ref, other_ref, copies):
         h_new.append(h)
         x_new.append(rms_norm(h, scale_ref[1, layer:layer + 1, :]))
     x = jnp.concatenate(x_new, axis=0)
-    ctx = cross_context(
+
+    def send_head(head, ctx):
+        ctx_ref[tp, head] = ctx.astype(BF16)
+        head_copy(ctx_ref, head, c_send, c_recv).start()
+
+    cross_context(
         x, mask_ref[...], wq_copy, wq_ref,
         lambda head: wait_all(k_in(head)), lambda head, slot: block(head * slots + slot)[...],
         lambda head: wait_all(v_in(head)), lambda head, slot: block((heads + head) * slots + slot)[...],
-        q_t, acc_ref, p_ref, ctx_t, True)
+        q_t, acc_ref, p_ref, send_head, True)
     for c in gate_up_in(g_slots - 1) + [down_in(d_slots - 1)]:
         c.start(priority=1)
-    wo_copy.wait()
-    send_projected(ctx, wo_ref, mine_ref, copies[1])
-    h_last, x_new = [], []
-    for h in receive_sum(h_new, mine_ref, other_ref.at[1], copies[1]):
-        h_last.append(h)
-        x_new.append(rms_norm(h, scale_ref[2, layer:layer + 1, :]))
-    h_float = jnp.concatenate(h_last, axis=0)
-    x = jnp.concatenate(x_new, axis=0)
+    mine = project_half(ctx_ref, full_ref, tp)
+    h_float = add_heads(jnp.concatenate(h_new, axis=0), mine, ctx_ref, full_ref, c_send, c_recv)
+    x = rms_norm(h_float, scale_ref[2, layer:layer + 1, :])
 
     def x_copy(expert, offset):
         return pltpu.make_async_remote_copy(
@@ -593,10 +615,9 @@
     gate = jnp.sum(logits_exp * onehot, axis=0, keepdims=True) / jnp.sum(logits_exp, axis=0, keepdims=True)
     gate_ref[...] = jnp.transpose(jnp.broadcast_to(gate, (tokens, tokens)))
 
-    def gate_up(expert):
-        slot = lax.rem(expert, g_slots)
+    def gate_up(expert, gate_ref, up_ref):
         x_rows = jnp.concatenate([recv_x[expert, g].astype(F32) for g in range(groups)], axis=0).astype(BF16)
-        return (jax.nn.gelu(dot(x_rows, eg_ref[slot])) * dot(x_rows, eu_ref[slot])).astype(BF16)
+        return (jax.nn.gelu(dot(x_rows, gate_ref[...])) * dot(x_rows, up_ref[...])).astype(BF16)
 
     def send_result(expert, y):
         for g in range(groups):
@@ -605,48 +626,81 @@
             y_copy(expert, number).start()
         recv_y[expert, me] = send_y[expert, ep]
 
+    streamed = local - lg_ref.shape[0]
+
     def wait_gate_up(expert):
         x_all(expert).wait_recv()
         for c in gate_up_in(expert):
             c.wait()
 
+    def streamed_gate_up(expert):
+        slot = lax.rem(expert, g_slots)
+        product_ref[lax.rem(expert, 2)] = gate_up(expert, eg_ref.at[slot], eu_ref.at[slot])
+
+    def streamed_down(expert):
+        return dot(product_ref[lax.rem(expert, 2)], ed_ref[lax.rem(expert, d_slots)]).astype(BF16)
+
     def collect(expert):
         y_all(expert).wait_recv()
         blocks = [recv_y[expert, g].astype(F32) + recv_y[expert, groups + g].astype(F32) for g in range(groups)]
         comb_ref[pl.ds(pl.multiple_of(expert * rows, rows), rows), :] = jnp.concatenate(blocks, axis=0).astype(BF16)
 
     wait_gate_up(0)
-    product_ref[0] = gate_up(0)
+    streamed_gate_up(0)
     for c in gate_up_in(g_slots):
         c.start(priority=1)
     lag = 4
+    turn = g_slots
+
+    def refill(expert):
+        @pl.when(expert + g_slots < streamed)
+        def _():
+            for c in gate_up_in(expert + g_slots):
+                c.start(priority=1)
+
+    def refill_down(expert):
+        @pl.when(expert + d_slots < streamed)
+        def _():
+            down_in(expert + d_slots).start(priority=1)
 
     def expert_step(expert, carry):
         wait_gate_up(expert)
         down_in(expert - 1).wait()
-        before = product_ref[lax.rem(expert - 1, 2)]
-        y = dot(before, ed_ref[lax.rem(expert - 1, d_slots)]).astype(BF16)
-        product_ref[lax.rem(expert, 2)] = gate_up(expert)
+        y = streamed_down(expert - 1)
+        streamed_gate_up(expert)
         send_result(expert - 1, y)
-
-        @pl.when(expert + g_slots < local)
+        refill(expert)
+        refill_down(expert - 1)
+
+        @pl.when(jnp.logical_and(expert >= lag, expert < turn))
         def _():
-            for c in gate_up_in(expert + g_slots):
-                c.start(priority=1)
-
-        @pl.when(expert - 1 + d_slots < local)
-        def _():
-            down_in(expert - 1 + d_slots).start(priority=1)
-
-        @pl.when(expert >= lag)
+            collect(expert - lag)
+
+        @pl.when(expert >= turn + lag)
         def _():
             collect(expert - lag)
         return carry
 
-    lax.fori_loop(1, local, expert_step, 0)
-    down_in(local - 1).wait()
-    send_result(local - 1, dot(product_ref[(local - 1) % 2], ed_ref[(local - 1) % d_slots]).astype(BF16))
-    for expert in range(local - lag, local):
+    lax.fori_loop(1, turn, expert_step, 0)
+    down_in(turn - 1).wait()
+    y = streamed_down(turn - 1)
+    before = turn - 1
+    for i in range(local - streamed):
+        x_all(streamed + i).wait_recv()
+        product_ref[2] = gate_up(streamed + i, lg_ref.at[i], lu_ref.at[i])
+        send_result(before, y)
+        if i == 0:
+            refill_down(turn - 1)
+        y = dot(product_ref[2], ld_ref[i]).astype(BF16)
+        before = streamed + i
+    wait_gate_up(turn)
+    streamed_gate_up(turn)
+    send_result(before, y)
+    refill(turn)
+    lax.fori_loop(turn + 1, streamed, expert_step, 0)
+    down_in(streamed - 1).wait()
+    send_result(streamed - 1, streamed_down(streamed - 1))
+    for expert in list(range(turn - lag, turn)) + list(range(streamed, local)) + list(range(streamed - lag, streamed)):
         collect(expert)
     combined = dot_t(place_ref[...], comb_ref[...])
     gate_col = gate_ref[...]
@@ -658,10 +712,10 @@
         y_all(expert).wait_send()
 
 
-def last(layer, h, part, mask, idx, scale, router, w_query, w_out, keys, values, exp_gate, exp_up, exp_down, groups):
+def last(layer, h, part, full, kept, mask, idx, scale, router, w_query, keys, values, exp_gate, exp_up, exp_down, groups):
     _, heads, slots, head_dim, tokens = keys.shape
     flat = keys.shape[:2] + (slots * head_dim, tokens)
-    width, model = w_out.shape[1:]
+    model, width = w_query.shape[1:]
     local, _, ff = exp_gate.shape
     experts = router.shape[0]
     capacity = (2 * tokens + experts - 1) // experts
@@ -672,7 +726,7 @@
     return pl.pallas_call(
         functools.partial(last_kernel, layer),
         out_shape=pltpu.VMEM((tokens, model), BF16),
-        in_specs=[vmem] * 2 + [hbm] * 11,
+        in_specs=[vmem] * 6 + [hbm] * 10,
         out_specs=vmem,
         scratch_shapes=[
             pltpu.VMEM(mask.shape, mask.dtype),
@@ -680,30 +734,28 @@
             pltpu.VMEM(scale.shape, F32),
             pltpu.VMEM(router.shape, F32),
             pltpu.VMEM((model, width), BF16),
-            pltpu.VMEM((width, model), BF16),
             pltpu.VMEM((GATE_SLOTS, model, ff), BF16),
             pltpu.VMEM((GATE_SLOTS, model, ff), BF16),
             pltpu.VMEM((DOWN_SLOTS, ff, model), BF16),
             pltpu.VMEM((heads, head_dim, tokens), F32),
             pltpu.VMEM((heads, slots * 8, tokens), F32),
             pltpu.VMEM((heads, slots, tokens), F32),
-            pltpu.VMEM((heads, head_dim, tokens), F32),
+            pltpu.VMEM((2, heads, head_dim, tokens), BF16),
             pltpu.VMEM((tokens, model), BF16),
-            pltpu.VMEM((2, tokens, model), BF16),
             pltpu.VMEM((experts * capacity, tokens), BF16),
             pltpu.VMEM((local, groups, capacity, model), BF16),
             pltpu.VMEM((local, groups, capacity, model), BF16),
-            pltpu.VMEM((2, groups * capacity, ff), BF16),
+            pltpu.VMEM((3, groups * capacity, ff), BF16),
             pltpu.VMEM((local, groups, capacity, model), BF16),
             pltpu.VMEM((local, 2 * groups, capacity, model), BF16),
             pltpu.VMEM((experts * capacity, model), BF16),
             pltpu.VMEM((tokens, tokens), F32),
-            dma((2,)), dma((heads, 4)), dma((heads, 4)), dma((GATE_SLOTS, 2)), dma((DOWN_SLOTS,)), dma((2, 2)), dma((2, 2)),
-            dma((local,)), dma((local,)), dma((local,)), dma((local,)), dma((4,)),
+            dma((1,)), dma((heads, 4)), dma((heads, 4)), dma((GATE_SLOTS, 2)), dma((DOWN_SLOTS,)), dma((2,)), dma((2,)),
+            dma((local,)), dma((local,)), dma((local,)), dma((local,)), dma((4,)), dma((heads,)), dma((heads,)),
         ],
         compiler_params=pltpu.CompilerParams(vmem_limit_bytes=LAST_VMEM, collective_id=1, has_side_effects=True),
         name="last",
-    )(on_chip(h), on_chip(part), *map(pinned, (mask, idx, scale, router, w_query, w_out, keys.reshape(flat), values.reshape(flat), exp_gate, exp_up, exp_down)))
+    )(*map(on_chip, (h, part, full, *kept)), *map(pinned, (mask, idx, scale, router, w_query, keys.reshape(flat), values.reshape(flat), exp_gate, exp_up, exp_down)))
 
 
 def decode_body(groups, hidden, write_pos, enc_mask, expert_idx, self_keys, self_values, cross_keys, cross_values, rel_bias, norm_scale, w_query, w_key, w_value, w_out, w_cross_query, w_cross_out, dense_gate, dense_up, dense_down, router, exp_gate, exp_up, exp_down):
@@ -715,11 +767,12 @@
     mask = jnp.transpose(enc_mask)
     scale = jnp.transpose(norm_scale, (1, 0, 2))
     keys, values, ckeys, cvalues = map(lanes, (self_keys, self_values, cross_keys, cross_values))
-    part, bias, k_out, v_first = self_first(0, hidden, pos, scale, rel_bias, w_query, w_key, w_value, w_out, keys, values)
-    following = (w_query, w_key, w_value, w_out, keys, values)
-    h, pos, scale_in, w_in, w_o, keys, values = middle(0, part, hidden, mask, scale, pos, w_cross_query, w_cross_out, ckeys, cvalues, dense_gate, dense_up, dense_down, following)
-    part, k_out, v_out = self_second(1, h, pos, scale_in, bias, w_in, w_o, keys, values, v_first, k_out)
-    h = last(1, h, part, mask, idx, scale, jnp.transpose(router), w_cross_query, w_cross_out, ckeys, cvalues, exp_gate, exp_up, exp_down, groups)
+    w_full = w_cross_out.reshape(w_cross_out.shape[0], groups, -1, w_cross_out.shape[2])
+    h, pos, scale_in, bias, w_in, w_o, keys, values, k_first, v_first, full, *kept = middle(
+        0, hidden, mask, scale, pos, rel_bias, (w_query, w_key, w_value, w_out), keys, values,
+        w_cross_query, w_cross_out, w_full, ckeys, cvalues, dense_gate, dense_up, dense_down, (exp_gate, exp_up, exp_down))
+    part, k_out, v_out = self_second(1, h, pos, scale_in, bias, w_in, w_o, keys, values, k_first, v_first)
+    h = last(1, h, part, full, kept, mask, idx, scale, jnp.transpose(router), w_cross_query, ckeys, cvalues, exp_gate, exp_up, exp_down, groups)
     return h, jnp.transpose(k_out, (0, 4, 1, 2, 3)), jnp.transpose(v_out, (0, 4, 1, 2, 3))
 
 

time: 76 us -> 74.3 us (0.978)
  Pallas kernels: 74.6 us -> 72.8 us
    pallas_call x1, Pallas kernels: 42.6 us -> 40.2 us  [last(): pl.pallas_call(functools.partial(last_kernel, layer), out_shape=pltpu.VME...]
    pallas_call x1, Pallas kernels: 3.86 us -> 4.73 us  [self_second(): pl.pallas_call(functools.partial(second_kernel, layer), out_shape=[pltpu....]
    pallas_call x2 -> x1, Pallas kernels: 28.1 us -> 27.9 us  [middle(): pl.pallas_call(functools.partial(middle_kernel, layer), out_shape=outs, i...]
where the time goes in v5:
time: 74.3 us; the launch traced here: 74.2 us
  Pallas kernels  72.8 us (98%)
    pallas_call x1, Pallas kernels, last(): pl.pallas_call(functools.partial(last_kernel, layer), out_shape=pltpu.VME...  40.2 us
    pallas_call x1, Pallas kernels, middle(): pl.pallas_call(functools.partial(middle_kernel, layer), out_shape=outs, i...  27.9 us
    pallas_call x1, Pallas kernels, self_second(): pl.pallas_call(functools.partial(second_kernel, layer), out_shape=[pltpu....  4.73 us

profile of v5, /device:TPU:0, one launch (start us, length us, event | category | flops | bytes accessed | tf_op | source)
XLA Modules:
  0.0 74.2 jit_solution(667231424982383889)
XLA Ops:
  0.6 27.9 %middle.1 = (bf16[128,768]{1,0:T(8,128)(2,1)S(1)}, s32[1,128]{1,0:T(1,128)S(1)}, f32[3,2,768]{2,1,0:T(2,128)S(1)}, f32[6,32,128]{2,1,0:T(8,128)S(1)}, bf16[3,768...) custom-call(bf16[128,768]{1,0:T(8,128)(2,1)} %h_hbm.1, ...), custom_call_target="tpu_custom_call" | custom-call | tf_op jit(solution)/shard_map/middle/pallas_call | solution.py:424
  28.6 4.7 %self_second.1 = (bf16[128,768]{1,0:T(8,128)(2,1)S(1)}, bf16[2,6,32,64,128]{4,3,2,1,0:T(8,128)(2,1)}, bf16[2,6,32,64,128]{4,3,2,1,0:T(8,128)(2,1)}) custom-call(bf16[128,768]{1,0:T(8,128)(2,1)S(1)} %get-tuple-element.20.h_ref, s32[1,128]{1,0:T(1,128)S(1)} %get-tuple-element.21.pos_ref, f32[3,2,768]{2,1,0:T(2,128)S(1)} %get-tuple-element.22.scale_ref, ...), custom_call_target="tpu_custom_call" | custom-call | tf_op jit(solution)/shard_map/self_second/pallas_call | solution.py:173
  33.3 40.2 %last.1 = bf16[128,768]{1,0:T(8,128)(2,1)S(1)} custom-call(bf16[128,768]{1,0:T(8,128)(2,1)S(1)} %get-tuple-element.20.h_ref, bf16[128,768]{1,0:T(8,128)(2,1)S(1)} %get-tuple-element.30.part_ref, bf16[2,4,96,768]{3,2,1,0:T(8,128)(2,1)S(1)} %get-tuple-element.31.full_ref, bf16[1,768,1536]{2,1,0:T(8,128)(2,1)S(1)} %get-tuple-element.32.lg_ref, ...), custom_call_target="tpu_custom_call" | custom-call | tf_op jit(solution)/shard_map/last/pallas_call | solution.py:726
  73.5 0.7 copy.27

commit v6 on v5

--- a/solution.py
+++ b/solution.py
@@ -328,13 +328,13 @@
     late = [pltpu.make_async_copy(s.at[first_kept + i], d.at[i], l_sem.at[i, j])
             for i in range(kept) for j, (s, d) in enumerate(((eg_hbm, lg_ref), (eu_hbm, lu_ref), (ed_hbm, ld_ref)))]
 
+    next_copy.start()
     for c in small + own[:3]:
         c.start()
     barrier = pltpu.get_barrier_semaphore()
     pl.semaphore_signal(barrier, inc=1, device_id={"tp": 1 - tp}, device_id_type=MESH)
     for offset in range(1, groups):
         pl.semaphore_signal(barrier, inc=1, device_id={"ep": lax.rem(ep + offset, groups)}, device_id_type=MESH)
-    next_copy.start()
     for head in range(heads):
         sk_in(head).start()
     for head in range(heads):
@@ -649,7 +649,7 @@
     streamed_gate_up(0)
     for c in gate_up_in(g_slots):
         c.start(priority=1)
-    lag = 4
+    lag = 5
     turn = g_slots
 
     def refill(expert):

time: 74.3 us -> 74.1 us (level)
  no operation moved by 1% of the time
where the time goes in v6:
time: 74.1 us; the launch traced here: 74 us
  Pallas kernels  72.7 us (98%)
    pallas_call x1, Pallas kernels, last(): pl.pallas_call(functools.partial(last_kernel, layer), out_shape=pltpu.VME...  39.8 us
    pallas_call x1, Pallas kernels, middle(): pl.pallas_call(functools.partial(middle_kernel, layer), out_shape=outs, i...  28.1 us
    pallas_call x1, Pallas kernels, self_second(): pl.pallas_call(functools.partial(second_kernel, layer), out_shape=[pltpu....  4.73 us

profile of v6, /device:TPU:0, one launch (start us, length us, event | category | flops | bytes accessed | tf_op | source)
XLA Modules:
  0.0 74.0 jit_solution(8898407757263249944)
XLA Ops:
  0.6 28.1 %middle.1 = (bf16[128,768]{1,0:T(8,128)(2,1)S(1)}, s32[1,128]{1,0:T(1,128)S(1)}, f32[3,2,768]{2,1,0:T(2,128)S(1)}, f32[6,32,128]{2,1,0:T(8,128)S(1)}, bf16[3,768...) custom-call(bf16[128,768]{1,0:T(8,128)(2,1)} %h_hbm.1, ...), custom_call_target="tpu_custom_call" | custom-call | tf_op jit(solution)/shard_map/middle/pallas_call | solution.py:424
  28.7 4.7 %self_second.1 = (bf16[128,768]{1,0:T(8,128)(2,1)S(1)}, bf16[2,6,32,64,128]{4,3,2,1,0:T(8,128)(2,1)}, bf16[2,6,32,64,128]{4,3,2,1,0:T(8,128)(2,1)}) custom-call(bf16[128,768]{1,0:T(8,128)(2,1)S(1)} %get-tuple-element.20.h_ref, s32[1,128]{1,0:T(1,128)S(1)} %get-tuple-element.21.pos_ref, f32[3,2,768]{2,1,0:T(2,128)S(1)} %get-tuple-element.22.scale_ref, ...), custom_call_target="tpu_custom_call" | custom-call | tf_op jit(solution)/shard_map/self_second/pallas_call | solution.py:173
  33.5 39.8 %last.1 = bf16[128,768]{1,0:T(8,128)(2,1)S(1)} custom-call(bf16[128,768]{1,0:T(8,128)(2,1)S(1)} %get-tuple-element.20.h_ref, bf16[128,768]{1,0:T(8,128)(2,1)S(1)} %get-tuple-element.30.part_ref, bf16[2,4,96,768]{3,2,1,0:T(8,128)(2,1)S(1)} %get-tuple-element.31.full_ref, bf16[1,768,1536]{2,1,0:T(8,128)(2,1)S(1)} %get-tuple-element.32.lg_ref, ...), custom_call_target="tpu_custom_call" | custom-call | tf_op jit(solution)/shard_map/last/pallas_call | solution.py:726
  73.3 0.7 copy.27
